TPU v7x, 256 devices: a whole 4x4x8 slice. The times are simulated.
256 devices in a mesh: gx: 8 (over z), gy: 32 (over x, y, core).
Axes of the slice: x: 4, y: 4, z: 8, core: 2. Of those that a mesh axis runs over, the one named last changes fastest.
Arguments:
- centres: bfloat16 [1048576, 256], P(('gx', 'gy')), may hold values from -20 to 20
- weights: float32 [16, 1048576], P(None, ('gx', 'gy')), may hold values from -0.375 to 0.375
- targets: float32 [16, 2048], P(None, ('gx', 'gy')), may hold values from -6 to 6
- batch_index: int32 [2048], P(('gx', 'gy')), may hold values from 0 to 1048575, as said below
- nystrom_index: int32 [16384], P(('gx', 'gy')), may hold values from 0 to 1048575, as said below
- eigvecs: float32 [16384, 128], P(('gx', 'gy')), may hold values from -0.046875 to 0.046875
- scales: float32 [128], replicated, may hold values from 0.2 to 2
Outputs:
- residual: float32 [16, 2048], P(None, ('gx', 'gy'))
- block_correction: float32 [16, 16384], P(None, ('gx', 'gy'))
Inputs may be any that keep to these rules, and one draw needn't show every extreme that they name: `batch_index`: the entries at positions j * 8 to (j + 1) * 8 - 1 name centres j * 4096 to (j + 1) * 4096 - 1, all different. `nystrom_index`: the entries at positions j * 64 to (j + 1) * 64 - 1 name centres j * 4096 to (j + 1) * 4096 - 1, all different.
All inputs are finite; a program needn't handle non-finite values.
Results may differ from a plain program's by a relative error of at most 0.0003.
Values may be sent and summed in bfloat16 or wider, within the bound.
No kernel may reach another device: no remote copies, remote signals or barrier semaphores. Data moves between devices by JAX's collectives and lax.ppermute only.
A program may use at most 192 MiB of HBM per device.

v0:
```python
import jax
import jax.numpy as jnp
from jax import lax
from jax.sharding import Mesh
from jax.sharding import PartitionSpec as P

GX_GY = ("gx", "gy_0", "gy_1", "gy_2")


def copy_for_each(x, axis):
    copies = jnp.broadcast_to(x, (lax.axis_size(axis), *x.shape))
    return lax.all_to_all(copies, axis, split_axis=0, concat_axis=0, tiled=True)


def of_everyone(x, axis):
    everything = copy_for_each(x, axis)
    return jnp.sum(everything, axis=0)


def over_axes(x, axes):
    far, near = axes
    return of_everyone(of_everyone(x, near), far)


def joined_along(parts, dim):
    parts = jnp.moveaxis(parts, 0, dim)
    shape = parts.shape
    return parts.reshape(*shape[:dim], shape[dim] * shape[dim + 1], *shape[dim + 2 :])


def gather_axes(x, axes, dim):
    far, near = axes
    parts = copy_for_each(copy_for_each(x, far), near)
    return joined_along(parts.swapaxes(0, 1).reshape(-1, *x.shape), dim)


def in_blocks(x, dim, peers):
    before, after = (x.shape[:dim], x.shape[dim + 1 :])
    return jnp.moveaxis(x.reshape(*before, peers, -1, *after), dim, 0)


def summed_on_arrival(x, axis, dim):
    peers = lax.axis_size(axis)
    parts = lax.all_to_all(in_blocks(x, dim, peers), axis, 0, 0, tiled=True)
    return jnp.sum(parts, axis=0)


def sum_in_two_steps(x, axes, dim):
    far, near = axes
    parts = in_blocks(x, dim, lax.axis_size(far))
    nearer = summed_on_arrival(parts, near, dim + 1)
    arrived = lax.all_to_all(nearer, far, split_axis=0, concat_axis=0, tiled=True)
    return arrived.sum(axis=0)


def kernel_tile(points, point_norm, others, other_norm):
    width = float(points.shape[1]) ** 0.5
    inner = jnp.dot(points, others.T, preferred_element_type=jnp.float32)
    squared = point_norm[:, None] + other_norm[None, :] - 2.0 * inner
    return jnp.exp(-jnp.sqrt(jnp.maximum(squared, 1.0)) / width)


def combine_projection(partial_projection):
    return over_axes(partial_projection, (("gx", "gy_0"), ("gy_1", "gy_2")))


def on_device(centres, weights, targets, batch_index, nystrom_index, eigvecs, scales):
    device_rank = lax.axis_index(GX_GY)
    local_count = centres.shape[0]
    outputs = weights.shape[0]
    local_batch = batch_index - device_rank * local_count
    local_block = nystrom_index - device_rank * local_count
    batch_local = jnp.take(centres, local_batch, axis=0)
    centre_norm = jnp.sum(centres.astype(jnp.float32) ** 2, axis=1)
    rows_in = gather_axes(batch_local, (("gx", "gy_0"), ("gy_1", "gy_2")), 0)
    rows_norm = jnp.sum(rows_in.astype(jnp.float32) ** 2, axis=1)
    tile = kernel_tile(rows_in, rows_norm, centres, centre_norm)
    predicted = lax.dot_general(
        weights, tile, (((1,), (1,)), ((), ())), precision=lax.Precision.HIGHEST
    )
    block_tile = jnp.take(tile, local_block, axis=1)
    carried = block_tile.T
    gathered = jnp.concatenate([predicted, carried], axis=0)
    partial_prediction = gathered[:outputs]
    carried = gathered[outputs:]
    reduced_cols = sum_in_two_steps(partial_prediction, (("gx", "gy_0"), ("gy_1", "gy_2")), 1)
    residual_local = reduced_cols - targets
    residual_full = gather_axes(residual_local, (("gx", "gy_0"), ("gy_1", "gy_2")), 1)
    along = jnp.dot(carried, residual_full.T, precision=lax.Precision.HIGHEST)
    projection = combine_projection(jnp.dot(eigvecs.T, along, precision=lax.Precision.HIGHEST))
    correction = jnp.dot(eigvecs * scales[None, :], projection, precision=lax.Precision.HIGHEST)
    return (residual_local, correction.T)


def solution(mesh):
    finer = Mesh(mesh.devices.reshape(mesh.shape["gx"], 4, 4, 2), ("gx", "gy_0", "gy_1", "gy_2"))
    in_specs = (
        P(GX_GY, None),
        P(None, GX_GY),
        P(None, GX_GY),
        P(GX_GY),
        P(GX_GY),
        P(GX_GY, None),
        P(),
    )
    out_specs = (P(None, GX_GY), P(None, GX_GY))
    return jax.shard_map(
        on_device, mesh=finer, in_specs=in_specs, out_specs=out_specs, check_vma=False
    )
```

profile of v0, /device:TPU:1, one launch (start us, length us, event | category | flops | bytes accessed | tf_op | source)
XLA Modules:
  0.0 220.2 jit_solution(4430987183101895627)
XLA Ops:
  0.6 0.0 copy-start
  0.7 0.7 compare_and_fusion.1
  1.4 2.4 %gather_fusion = bf16[8,256]{1,0:T(8,128)(2,1)S(1)} fusion(bf16[4096,256]{1,0:T(8,128)(2,1)} %param.7, s32[1024]{0:T(1024)S(1)} %pad_clamp_fusion.1), kind=kCustom, calls=%fused_computation | custom fusion | bytes 8224 | tf_op jit(solution)/shard_map/jit(_take)/gather | solution.py:73
  3.8 0.1 broadcast_select_fusion
  3.9 21.0 %all_to_all.40 = bf16[32,8,256]{2,1,0:T(8,128)(2,1)S(1)} all-to-all(bf16[32,8,256]{2,1,0:T(8,128)(2,1)S(1)} %broadcast_in_dim.48), channel_id=1, replica_groups=mesh['gx'=8,'gy_0'=4,'gy_1'=4,'gy_2'=2] {'gx','gy_0'}, dimensions={0} | all-to-all | bytes 262144 | tf_op jit(solution)/shard_map/all_to_all | solution.py:12
  24.9 1.1 broadcast_in_dim.49
  25.9 6.5 %all-to-all-start.1 = ((bf16[8,32,8,256]{3,2,1,0:T(8,128)(2,1)}), bf16[8,32,8,256]{3,2,1,0:T(8,128)(2,1)S(1)}, u32[]{:S(2)}, u32[]{:S(2)}) async-start(bf16[8,32,8,256]{3,2,1,0:T(8,128)(2,1)} %broadcast_in_dim.49), calls=%async_computation.1 | async-start | bytes 2097152 | tf_op jit(solution)/shard_map/all_to_all | solution.py:12
  32.5 2.2 %multiply_reduce_fusion = f32[4096]{0:T(1024)S(1)} fusion(bf16[4096,256]{1,0:T(8,128)(2,1)} %param.7), kind=kLoop, calls=%fused_computation.3 | loop fusion | flops 3141632 | bytes 2113536 | tf_op jit(solution)/shard_map/reduce_sum | solution.py:74
  34.7 12.8 %all-to-all-done.1 = bf16[8,32,8,256]{3,2,1,0:T(8,128)(2,1)S(1)} async-done(((bf16[8,32,8,256]{3,2,1,0:T(8,128)(2,1)}), bf16[8,32,8,256]{3,2,1,0:T(8,128)(2,1)S(1)}, u32[]{:S(2)}, u32[]{:S(2)}) %all-to-all-start.1) | async-done | bytes 1048608 | tf_op jit(solution)/shard_map/all_to_all | solution.py:12
  47.4 0.3 multiply_reduce_fusion.1
  47.8 0.1 add.40
  47.9 0.1 copy.32
  48.0 22.3 %multiply_exponential_fusion = f32[2048,4096]{1,0:T(8,128)} fusion(f32[4096]{0:T(1024)S(1)} %multiply_reduce_fusion, f32[2048]{0:T(1024)S(1)} %add.40, bf16[2048,256]{1,0:T(8,128)(2,1)S(1)} %bitcast.45, bf16[4096,256]{1,0:T(8,128)(2,1)} %param.7), kind=kOutput, calls=%fused_computation.2 | convolution fusion | flops 4345298944 | bytes 36724736 | tf_op jit(solution)/shard_map/dot_general | solution.py:58
  70.3 0.0 copy-done
  70.3 0.0 copy-start.3
  70.3 0.0 copy-start.5
  70.3 32.0 %convolution_bitcast_fusion = f32[16,2048]{1,0:T(8,128)S(1)} fusion(f32[2048,4096]{1,0:T(8,128)} %multiply_exponential_fusion, f32[16,4096]{1,0:T(8,128)S(1)} %copy-done), kind=kOutput, calls=%fused_computation.4 | convolution fusion | flops 1610612736 | bytes 33947648 | tf_op jit(solution)/shard_map/dot_general | solution.py:78
  102.3 0.1 reshape.31
  102.5 0.2 copy.33
  102.7 0.3 reshape.53
  103.0 8.6 %all_to_all.41 = f32[8,1,4096]{2,1,0:T(1,128)S(1)} all-to-all(f32[8,1,4096]{2,1,0:T(1,128)S(1)} %reshape.53), channel_id=1, replica_groups=mesh['gx'=8,'gy_0'=4,'gy_1'=4,'gy_2'=2] {'gy_1','gy_2'}, dimensions={0} | all-to-all | bytes 262144 | tf_op jit(solution)/shard_map/all_to_all | solution.py:44
  111.5 0.5 broadcast.36
  112.0 1.0 reduce.1
  113.0 0.2 reshape.54
  113.2 0.1 copy.36
  113.3 0.1 reshape.55
  113.5 11.7 %all_to_all.42 = f32[32,1,128]{2,1,0:T(1,128)S(1)} all-to-all(f32[32,1,128]{2,1,0:T(1,128)S(1)} %reshape.55), channel_id=1, replica_groups=mesh['gx'=8,'gy_0'=4,'gy_1'=4,'gy_2'=2] {'gx','gy_0'}, dimensions={0} | all-to-all | bytes 32768 | tf_op jit(solution)/shard_map/all_to_all | solution.py:52
  125.2 0.7 reduce.2
  125.8 0.1 reshape.56
  126.0 0.0 copy-done.3
  126.0 0.0 copy-start.2
  126.0 0.1 reshape.57
  126.1 11.6 %all_to_all.43 = f32[32,1,128]{2,1,0:T(1,128)S(1)} all-to-all(f32[32,1,128]{2,1,0:T(1,128)S(1)} %reshape.57), channel_id=1, replica_groups=mesh['gx'=8,'gy_0'=4,'gy_1'=4,'gy_2'=2] {'gx','gy_0'}, dimensions={0} | all-to-all | bytes 32768 | tf_op jit(solution)/shard_map/all_to_all | solution.py:12
  137.7 0.7 reduce.3
  138.4 0.1 reshape.58
  138.5 0.1 copy.38
  138.7 0.9 reshape.59
  139.6 6.7 %all-to-all-start.5 = ((f32[8,1,4096]{2,1,0:T(1,128)}), f32[8,1,4096]{2,1,0:T(1,128)S(1)}, u32[]{:S(2)}, u32[]{:S(2)}) async-start(f32[8,1,4096]{2,1,0:T(1,128)} %reshape.59), calls=%async_computation.5 | async-start | bytes 262144 | tf_op jit(solution)/shard_map/all_to_all | solution.py:12
  146.3 0.0 copy-done.5
  146.3 0.0 copy-start.1
  146.3 0.0 copy-start.4
  146.3 33.4 %copy.37 = f32[2048,4096]{0,1:T(8,128)} copy(f32[2048,4096]{1,0:T(8,128)} %multiply_exponential_fusion) | data formatting | bytes 67108864 | tf_op jit(solution)/shard_map/exp | solution.py:60
  179.7 0.0 copy-done.2
  179.7 11.5 %gather_fusion.1 = f32[64,2048]{1,0:T(8,128)S(1)} fusion(f32[2048,4096]{0,1:T(8,128)} %copy.37, s32[1024]{0:T(1024)S(1)} %pad_clamp_fusion), kind=kCustom, calls=%fused_computation.1 | custom fusion | bytes 1048832 | tf_op jit(solution)/shard_map/jit(_take)/gather | solution.py:81
  191.3 0.0 all-to-all-done.5
  191.3 1.0 reduce.4
  192.2 0.2 reshape.60
  192.5 0.9 copy.39
  193.4 1.8 fusion
  195.2 0.0 copy-done.1
  195.2 0.1 convolution_bitcast_fusion.1
  195.4 9.5 %all_to_all.44 = f32[8,128,16]{1,2,0:T(8,128)S(1)} all-to-all(f32[8,128,16]{1,2,0:T(8,128)S(1)} %broadcast_in_dim.55), channel_id=1, replica_groups=mesh['gx'=8,'gy_0'=4,'gy_1'=4,'gy_2'=2] {'gy_1','gy_2'}, dimensions={0} | all-to-all | bytes 131072 | tf_op jit(solution)/shard_map/all_to_all | solution.py:12
  204.9 14.5 %all_to_all.45 = f32[32,128,16]{1,2,0:T(8,128)S(1)} all-to-all(f32[32,128,16]{1,2,0:T(8,128)S(1)} %broadcast_in_dim.56), channel_id=1, replica_groups=mesh['gx'=8,'gy_0'=4,'gy_1'=4,'gy_2'=2] {'gx','gy_0'}, dimensions={0} | all-to-all | bytes 524288 | tf_op jit(solution)/shard_map/all_to_all | solution.py:12
  219.4 0.0 copy-done.4
  219.4 0.8 fusion.4
  (15 shorter events, 0.3 us)
Async XLA Ops:
  0.6 69.7 %copy-start = (f32[16,4096]{1,0:T(8,128)S(1)}, f32[16,4096]{1,0:T(8,128)}, u32[]{:S(2)}) copy-start(f32[16,4096]{1,0:T(8,128)} %param.8) | copy-start | bytes 786436
  25.9 21.5 %all-to-all-start.1 = ((bf16[8,32,8,256]{3,2,1,0:T(8,128)(2,1)}), bf16[8,32,8,256]{3,2,1,0:T(8,128)(2,1)S(1)}, u32[]{:S(2)}, u32[]{:S(2)}) async-start(bf16[8,32,8,256]{3,2,1,0:T(8,128)(2,1)} %broadcast_in_dim.49), calls=%async_computation.1 | async-start | bytes 2097152 | tf_op jit(solution)/shard_map/all_to_all | solution.py:12
  70.3 55.7 %copy-start.3 = (f32[16,8]{0,1:T(8,128)S(1)}, f32[16,8]{0,1:T(8,128)}, u32[]{:S(2)}) copy-start(f32[16,8]{0,1:T(8,128)} %param.9) | copy-start | bytes 1540
  70.3 76.0 %copy-start.5 = (s32[64]{0:T(128)S(1)}, s32[64]{0:T(128)}, u32[]{:S(2)}) copy-start(s32[64]{0:T(128)} %param.11) | copy-start | bytes 772
  126.0 53.7 %copy-start.2 = (f32[16,8]{0,1:T(8,128)}, f32[16,8]{0,1:T(8,128)S(1)}, u32[]{:S(2)}) copy-start(f32[16,8]{0,1:T(8,128)S(1)} %sub.21) | copy-start | bytes 1540
  139.6 51.7 %all-to-all-start.5 = ((f32[8,1,4096]{2,1,0:T(1,128)}), f32[8,1,4096]{2,1,0:T(1,128)S(1)}, u32[]{:S(2)}, u32[]{:S(2)}) async-start(f32[8,1,4096]{2,1,0:T(1,128)} %reshape.59), calls=%async_computation.5 | async-start | bytes 262144 | tf_op jit(solution)/shard_map/all_to_all | solution.py:12
  146.3 48.9 %copy-start.1 = (f32[64,128]{1,0:T(8,128)S(1)}, f32[64,128]{1,0:T(8,128)}, u32[]{:S(2)}) copy-start(f32[64,128]{1,0:T(8,128)} %param.12) | copy-start | bytes 98308
  146.3 73.1 %copy-start.4 = (f32[128]{0:T(128)S(1)}, f32[128]{0:T(128)}, u32[]{:S(2)}) copy-start(f32[128]{0:T(128)} %param.13) | copy-start | bytes 1540
where the time goes:
time: 221 us; the launch traced here: 220 us
  blocking collectives  76.8 us (35%)
  matrix products  57 us (26%)
  local copies, waits for them, and re-layouts  52.7 us (24%)
  starting transfers between devices  13.2 us (6%)
  waiting for transfers between devices  12.8 us (6%)
  other arithmetic  6.75 us (3%)
    all_to_all x4, blocking collectives, copy_for_each(): return lax.all_to_all(copies, axis, split_axis=0, concat_axis=0, tiled=True)  56.5 us
    exp x1, local copies, waits for them, and re-layouts, kernel_tile(): return jnp.exp(-jnp.sqrt(jnp.maximum(squared, 1.0)) / width)  33.4 us
    dot_general x1, matrix products, on_device(): lax.dot_general(weights, tile, (((1,), (1,)), ((), ())), precision=lax.Pr...  32 us
    dot_general x1, matrix products, kernel_tile(): inner = jnp.dot(points, others.T, preferred_element_type=jnp.float32)  22.3 us
    all_to_all x2, starting transfers between devices, copy_for_each(): return lax.all_to_all(copies, axis, split_axis=0, concat_axis=0, tiled=True)  13.2 us
    all_to_all x2, waiting for transfers between devices, copy_for_each(): return lax.all_to_all(copies, axis, split_axis=0, concat_axis=0, tiled=True)  12.8 us
    all_to_all x1, blocking collectives, sum_in_two_steps(): lax.all_to_all(nearer, far, split_axis=0, concat_axis=0, tiled=True)  11.7 us
    gather x1, local copies, waits for them, and re-layouts, on_device(): block_tile = jnp.take(tile, local_block, axis=1)  11.5 us
  transfers between devices with their start and end apart: 2, of which 1 were waited for; matrix products, arithmetic and copies ran while one was open for 21% of the time, Pallas kernels for 0%

commit v1 on v0

v1 whole, which is shorter than its diff:
```python
import math

import jax
import jax.numpy as jnp
from jax import lax
from jax.experimental import pallas as pl
from jax.experimental.pallas import tpu as pltpu
from jax.sharding import Mesh
from jax.sharding import PartitionSpec as P

ALL = ("z", "x", "y", "c")
PLANE = ("x", "y")
COLUMN = ("z", "c")
CHUNK = 256
NT = (((1,), (1,)), ((), ()))
NN = (((1,), (0,)), ((), ()))
VMEM_LIMIT = 48 * 1024 * 1024


def split(v):
    hi = v.astype(jnp.bfloat16)
    lo = (v - hi.astype(jnp.float32)).astype(jnp.bfloat16)
    return hi, lo


def mxu(a, b, dims):
    return lax.dot_general(a, b, dims, preferred_element_type=jnp.float32)


def dot_f32(a, b, dims):
    rows = a.shape[0]
    both = jnp.concatenate(split(a), axis=0)
    b_hi, b_lo = split(b)
    out = mxu(both, b_hi, dims) + mxu(both, b_lo, dims)
    return out[:rows] + out[rows:]


def squares(v):
    wide = v.astype(jnp.float32)
    return split(wide * wide)


def pick_kernel(first_ref, batch_ref, block_ref, centres_ref, rows_ref, points_ref):
    count = centres_ref.shape[0]
    first = first_ref[0]
    sub = lax.broadcasted_iota(jnp.int32, (8, 128), 0)
    lane = lax.broadcasted_iota(jnp.int32, (8, 128), 1)

    def wanted(ref, start):
        tile = jnp.zeros((8, 128), jnp.int32)
        for r in range(8):
            tile = jnp.where(sub == r, ref[start + r] - first, tile)
        return tile

    groups = [wanted(batch_ref, 0)]
    for start in range(0, block_ref.shape[0], 8):
        groups.append(wanted(block_ref, start))
    found = jnp.zeros((8 * len(groups), centres_ref.shape[1]), jnp.float32)
    for base in range(0, count, CHUNK):
        pieces = []
        for tile in groups:
            halves = [
                jnp.where(tile == lane + (base + k), 1.0, 0.0) for k in range(0, CHUNK, 128)
            ]
            pieces.append(jnp.concatenate(halves, axis=1))
        hot = jnp.concatenate(pieces, axis=0).astype(jnp.bfloat16)
        found = found + mxu(hot, centres_ref[base : base + CHUNK, :], NN)
    batch = found[:8].astype(jnp.bfloat16)
    rows_ref[...] = jnp.broadcast_to(batch[None], rows_ref.shape)
    points_ref[...] = found[8:].astype(jnp.bfloat16)


def prepare_kernel(centres_ref, points_ref, weights_ref, norm_ref, point_norm_ref, terms_ref):
    ones = jnp.ones((centres_ref.shape[1], 128), jnp.bfloat16)

    def norms(v):
        hi, lo = squares(v)
        return mxu(hi, ones, NN) + mxu(lo, ones, NN)

    for base in range(0, centres_ref.shape[0], CHUNK):
        norm_ref[base : base + CHUNK, :] = norms(centres_ref[base : base + CHUNK, :])
    point_norm_ref[...] = norms(points_ref[...])
    terms_ref[...] = jnp.concatenate(split(weights_ref[...]), axis=0)


def tile_kernel(
    core_ref, own_ref, other_ref, centres_ref, norm_ref, terms_ref, points_ref, point_norm_ref,
    out_ref, block_hi_ref, block_lo_ref,
):
    depth = centres_ref.shape[1]
    pieces = []
    for h in range(2):
        pieces.append(own_ref[:, h].reshape(-1, depth))
        pieces.append(other_ref[:, h].reshape(-1, depth))
    rows = jnp.concatenate(pieces, axis=0)
    hi, lo = squares(rows)
    ones = jnp.ones((8, depth), jnp.bfloat16)
    row_norm = (mxu(ones, hi, NT) + mxu(ones, lo, NT))[:1]
    doubled = rows * jnp.bfloat16(-2.0)
    factor = -1.0 / (float(depth) ** 0.5 * math.log(2.0))

    def kernel_values(v, v_norm):
        inner = mxu(v, doubled, NT)
        wide = jnp.concatenate([v_norm, v_norm], axis=1)
        squared = jnp.maximum((wide + row_norm) + inner, 1.0)
        return jnp.exp2(squared * lax.rsqrt(squared) * factor)

    total = jnp.zeros((terms_ref.shape[0], rows.shape[0]), jnp.float32)
    for base in range(0, centres_ref.shape[0], CHUNK):
        values = kernel_values(
            centres_ref[base : base + CHUNK, :], norm_ref[base : base + CHUNK, :]
        )
        k_hi, k_lo = split(values)
        terms = terms_ref[:, base : base + CHUNK]
        total = total + mxu(terms, k_hi, NN)
        total = total + mxu(terms, k_lo, NN)
    outputs = total.shape[0] // 2
    predicted = total[:outputs] + total[outputs:]
    block = kernel_values(points_ref[...], point_norm_ref[...])
    swapped = core_ref[0] == 1

    def ordered(v):
        return jnp.where(swapped, pltpu.roll(v, 64, 1), v)

    for h in range(2):
        out_ref[h] = ordered(predicted[:, h * 128 : (h + 1) * 128])
        b_hi, b_lo = split(ordered(block[:, h * 128 : (h + 1) * 128]))
        block_hi_ref[:, h * 128 : (h + 1) * 128] = b_hi
        block_lo_ref[:, h * 128 : (h + 1) * 128] = b_lo


def combine_kernel(parts_ref, less_ref, out_ref):
    total = jnp.sum(parts_ref[...], axis=0) - less_ref[...]
    out_ref[...] = jnp.broadcast_to(total[None], out_ref.shape)


def spread_kernel(parts_ref, out_ref):
    total = jnp.sum(parts_ref[...], axis=0)
    out_ref[...] = jnp.broadcast_to(total[None], out_ref.shape)


def project_kernel(residual_ref, block_hi_ref, block_lo_ref, vectors_ref, out_ref):
    residual = jnp.concatenate([residual_ref[h] for h in range(residual_ref.shape[0])], axis=1)
    rows = residual.shape[0]
    both = jnp.concatenate(split(residual), axis=0)
    along = mxu(both, block_hi_ref[...], NT) + mxu(both, block_lo_ref[...], NT)
    along = along[:rows] + along[rows:]
    projection = dot_f32(along, vectors_ref[...], NN)
    out_ref[...] = jnp.broadcast_to(projection[None], out_ref.shape)


def correct_kernel(parts_ref, scales_ref, vectors_ref, out_ref):
    projection = jnp.sum(parts_ref[...], axis=0) * scales_ref[...]
    out_ref[...] = dot_f32(projection, vectors_ref[...], NT)


def call(kernel, out, *args, **kwargs):
    return pl.pallas_call(
        kernel,
        out_shape=out,
        compiler_params=pltpu.CompilerParams(vmem_limit_bytes=VMEM_LIMIT),
        **kwargs,
    )(*args)


def shape(dims, dtype=jnp.float32):
    return jax.ShapeDtypeStruct(dims, dtype)


def exchange(x, axes):
    return lax.all_to_all(x, axes, split_axis=0, concat_axis=0, tiled=True)


def on_device(centres, weights, targets, batch_index, nystrom_index, eigvecs, scales):
    count, depth = centres.shape
    outputs = weights.shape[0]
    own = batch_index.shape[0]
    block = nystrom_index.shape[0]
    sizes = {a: lax.axis_size(a) for a in ALL}
    plane = sizes["x"] * sizes["y"]
    chips = sizes["z"] * plane
    column = sizes["z"] * sizes["c"]
    first = (lax.axis_index(ALL) * count).astype(jnp.int32).reshape(1)
    core = lax.axis_index("c").astype(jnp.int32).reshape(1)
    place = lax.axis_index("c") * sizes["z"] + lax.axis_index("z")
    smem = pl.BlockSpec(memory_space=pltpu.SMEM)
    vmem = pl.BlockSpec(memory_space=pltpu.VMEM)

    rows, points = call(
        pick_kernel,
        (shape((chips, own, depth), jnp.bfloat16), shape((block, depth), jnp.bfloat16)),
        first, batch_index, nystrom_index, centres,
        in_specs=[smem, smem, smem, vmem],
        out_specs=(vmem, vmem),
    )
    mine = exchange(rows, ("z", "x", "y")).reshape(sizes["z"], plane, own, depth)
    norm, point_norm, terms = call(
        prepare_kernel,
        (shape((count, 128)), shape((block, 128)), shape((2 * outputs, count), jnp.bfloat16)),
        centres, points, weights,
    )
    other = lax.ppermute(mine, "c", [(0, 1), (1, 0)])

    whole = lambda *dims: pl.BlockSpec(dims, lambda i: (0,) * len(dims))
    rows_spec = pl.BlockSpec((sizes["z"], 2, own, depth), lambda i: (0, i, 0, 0))
    batch = plane * 128
    predicted, block_hi, block_lo = call(
        tile_kernel,
        (
            shape((plane, outputs, 128)),
            shape((block, batch), jnp.bfloat16),
            shape((block, batch), jnp.bfloat16),
        ),
        core, mine, other, centres, norm, terms, points, point_norm,
        grid=(plane // 2,),
        in_specs=[
            smem, rows_spec, rows_spec, whole(count, depth), whole(count, 128),
            whole(2 * outputs, count), whole(block, depth), whole(block, 128),
        ],
        out_specs=(
            pl.BlockSpec((2, outputs, 128), lambda i: (i, 0, 0)),
            pl.BlockSpec((block, 256), lambda i: (0, i)),
            pl.BlockSpec((block, 256), lambda i: (0, i)),
        ),
    )
    lanes = lax.broadcasted_iota(jnp.int32, (outputs, 128), 1) // own
    less = jnp.where(lanes == place, jnp.tile(targets, (1, 128 // own)), 0.0)
    gathered = exchange(predicted, PLANE)
    summed = call(combine_kernel, shape((column, outputs, 128)), gathered, less)
    summed = exchange(summed, COLUMN)
    residual = call(spread_kernel, shape((plane, outputs, 128)), summed)
    residual_local = lax.dynamic_slice(residual, (0, 0, place * own), (1, outputs, own))[0]
    residual = exchange(residual, PLANE)
    projection = call(
        project_kernel, shape((plane, outputs, 128)), residual, block_hi, block_lo, eigvecs
    )
    projection = exchange(projection, PLANE)
    projection = call(spread_kernel, shape((column, outputs, 128)), projection)
    projection = exchange(projection, COLUMN)
    correction = call(
        correct_kernel, shape((outputs, block)), projection, scales[None, :], eigvecs
    )
    return residual_local, correction


def solution(mesh):
    finer = Mesh(mesh.devices.reshape(mesh.shape["gx"], 4, 4, 2), ALL)
    in_specs = (
        P(ALL, None),
        P(None, ALL),
        P(None, ALL),
        P(ALL),
        P(ALL),
        P(ALL, None),
        P(),
    )
    out_specs = (P(None, ALL), P(None, ALL))
    return jax.shard_map(
        on_device, mesh=finer, in_specs=in_specs, out_specs=out_specs, check_vma=False
    )
```

time: 221 us -> 126 us (0.57)
  matrix products: 57 us -> 0 us
  local copies, waits for them, and re-layouts: 52.7 us -> 7.34 us
  Pallas kernels: 0 us -> 22.6 us
  blocking collectives: 76.8 us -> 67.6 us
  other arithmetic: 6.75 us -> 0.02 us
  waiting for transfers between devices: 12.8 us -> 15.1 us
    dot_general x5 -> x0, matrix products: 57 us -> none  [the longest x1 32 us: on_device(): lax.dot_general(weights, tile, (((1,), (1,)), ((), ())), precision=lax.Pr...]
    exp x1 -> x0, local copies, waits for them, and re-layouts: 33.4 us -> none  [kernel_tile(): return jnp.exp(-jnp.sqrt(jnp.maximum(squared, 1.0)) / width)]
    pallas_call x0 -> x8, Pallas kernels: none -> 22.6 us  [call(): pl.pallas_call(kernel, out_shape=out, compiler_params=pltpu.CompilerParam...]
    gather x2 -> x0, local copies, waits for them, and re-layouts: 14 us -> none  [the longest x1 11.5 us: on_device(): block_tile = jnp.take(tile, local_block, axis=1)]
    all_to_all x6 -> x4, blocking collectives: 76.8 us -> 67.6 us  [exchange(): return lax.all_to_all(x, axes, split_axis=0, concat_axis=0, tiled=True)]
    unnamed x23 -> x24, local copies, waits for them, and re-layouts: 2 us -> 6.55 us
    all_to_all x2, starting transfers between devices: 13.2 us -> 9.37 us  [exchange(): return lax.all_to_all(x, axes, split_axis=0, concat_axis=0, tiled=True)]
    all_to_all x4 -> x0, other arithmetic: 3.27 us -> none  [the longest x2 1.64 us: copy_for_each(): return lax.all_to_all(copies, axis, split_axis=0, concat_axis=0, tiled=True)]
  transfers between devices with their start and end apart: 2 -> 3, of which waited for: 1 -> 2; matrix products, arithmetic and copies ran while one was open for 21% -> 1% of each run, Pallas kernels for 0% -> 1%
where the time goes in v1:
time: 126 us
  blocking collectives  67.6 us (54%)
  Pallas kernels  22.6 us (18%)
  waiting for transfers between devices  15.1 us (12%)
  starting transfers between devices  12.5 us (10%)
  local copies, waits for them, and re-layouts  7.34 us (6%)
    all_to_all x4, blocking collectives, exchange(): return lax.all_to_all(x, axes, split_axis=0, concat_axis=0, tiled=True)  67.6 us
    pallas_call x8, Pallas kernels, call(): pl.pallas_call(kernel, out_shape=out, compiler_params=pltpu.CompilerParam...  22.6 us
    all_to_all x2, waiting for transfers between devices, exchange(): return lax.all_to_all(x, axes, split_axis=0, concat_axis=0, tiled=True)  15.1 us
    all_to_all x2, starting transfers between devices, exchange(): return lax.all_to_all(x, axes, split_axis=0, concat_axis=0, tiled=True)  9.37 us
    unnamed x24, local copies, waits for them, and re-layouts  6.55 us
    ppermute x1, starting transfers between devices, on_device(): other = lax.ppermute(mine, 'c', [(0, 1), (1, 0)])  3.09 us
  transfers between devices with their start and end apart: 3, of which 2 were waited for; matrix products, arithmetic and copies ran while one was open for 1% of the time, Pallas kernels for 1%

profile of v1, /device:TPU:1, one launch (start us, length us, event | category | flops | bytes accessed | tf_op | source)
XLA Modules:
  0.0 125.9 jit_solution(16569802675053235072)
XLA Ops:
  0.6 0.0 copy-start
  0.7 0.0 copy-start.1
  0.7 1.6 %copy-done.1 = bf16[4096,256]{1,0:T(8,128)(2,1)S(1)} copy-done((bf16[4096,256]{1,0:T(8,128)(2,1)S(1)}, bf16[4096,256]{1,0:T(8,128)(2,1)}, u32[]{:S(2)}) %copy-start.1) | copy-done | bytes 2097176
  2.3 0.0 copy-start.9
  2.3 0.7 copy-done.9
  2.9 0.0 copy-start.10
  2.9 0.7 copy-done.10
  3.6 0.0 copy-start.2
  3.6 0.0 copy-start.4
  3.6 1.0 shard_map.86
  4.6 34.7 %all_to_all.30 = bf16[128,8,256]{2,1,0:T(8,128)(2,1)S(1)} all-to-all(bf16[128,8,256]{2,1,0:T(8,128)(2,1)S(1)} %get-tuple-element.10), channel_id=1, replica_groups=mesh['z'=8,'x'=4,'y'=4,'c'=2] {'z','x','y'}, dimensions={0} | all-to-all | bytes 1048576 | tf_op jit(solution)/shard_map/all_to_all | solution.py:171
  39.3 3.1 %collective-permute-start = (bf16[8,16,8,256]{3,2,1,0:T(8,128)(2,1)S(1)}, bf16[8,16,8,256]{3,2,1,0:T(8,128)(2,1)S(1)}, u32[]{:S(2)}, u32[]{:S(2)}) collective-permute-start(bf16[8,16,8,256]{3,2,1,0:T(8,128)(2,1)S(1)} %bitcast.7), channel_id=1, source_target_pairs={{0,1},{1,0},{2,3},{3,2},{4,5},{5,4},{6,7},{7,6},{8,9},{9,8},{10,11... | collective-permute-start | bytes 1572872 | tf_op jit(solution)/shard_map/ppermute | solution.py:202
  42.4 0.0 copy-done
  42.4 0.1 copy.11
  42.4 0.0 copy-done.2
  42.4 0.0 copy-done.4
  42.4 1.3 %shard_map.87 = (f32[4096,128]{1,0:T(8,128)S(1)}, f32[64,128]{1,0:T(8,128)S(1)}, bf16[32,4096]{1,0:T(8,128)(2,1)S(1)}) custom-call(bf16[4096,256]{1,0:T(8,128)(2,1)S(1)} %copy-done.2, bf16[64,256]{1,0:T(8,128)(2,1)S(1)} %get-tuple-element.11.points_ref, f32[16,4096]{1,0:T(8,128)S(1)} %copy-done.4), custom_call_target="tpu_custom_call" | custom-call | tf_op jit(solution)/shard_map/pallas_call | solution.py:158
  43.7 0.0 copy-start.3
  43.7 1.3 %copy-done.3 = f32[4096,128]{1,0:T(8,128)} copy-done((f32[4096,128]{1,0:T(8,128)}, f32[4096,128]{1,0:T(8,128)S(1)}, u32[]{:S(2)}) %copy-start.3) | copy-done | bytes 2097176
  45.1 0.0 collective-permute-done.other_ref
  45.1 0.0 copy-start.8
  45.1 18.4 %shard_map.88 = (f32[16,16,128]{2,1,0:T(8,128)S(1)}, bf16[64,2048]{1,0:T(8,128)(2,1)S(1)}, bf16[64,2048]{1,0:T(8,128)(2,1)S(1)}) custom-call(s32[1]{0:T(128)} %bitcast.core_ref, bf16[8,16,8,256]{3,2,1,0:T(8,128)(2,1)S(1)} %bitcast.8, bf16[8,16,8,256]{3,2,1,0:T(8,128)(2,1)S(1)} %collective-permute-done.other_ref, bf16[4096,256]{1,0:T(8,128)(2,1)S(1)} %copy-done.2, ...), custom_call_target="tpu_custom_call" | custom-call | tf_op jit(solution)/shard_map/pallas_call | solution.py:158
  63.5 0.0 copy-start.5
  63.5 0.7 copy-done.5
  64.2 0.0 copy-start.7
  64.2 0.6 copy-done.7
  64.8 0.0 copy-start.11
  64.8 3.6 %all-to-all-start.1 = ((f32[16,16,128]{2,1,0:T(8,128)}), f32[16,16,128]{2,1,0:T(8,128)S(1)}, u32[]{:S(2)}, u32[]{:S(2)}) async-start(f32[16,16,128]{2,1,0:T(8,128)} %copy-done.7), calls=%async_computation.1 | async-start | bytes 262144 | tf_op jit(solution)/shard_map/all_to_all | solution.py:171
  68.5 6.7 %all-to-all-done.1.parts_ref = f32[16,16,128]{2,1,0:T(8,128)S(1)} async-done(((f32[16,16,128]{2,1,0:T(8,128)}), f32[16,16,128]{2,1,0:T(8,128)S(1)}, u32[]{:S(2)}, u32[]{:S(2)}) %all-to-all-start.1) | async-done | bytes 131104 | tf_op jit(solution)/shard_map/all_to_all | solution.py:171
  75.2 12.9 %all_to_all.31.parts_ref = f32[16,16,128]{2,1,0:T(8,128)S(1)} all-to-all(f32[16,16,128]{2,1,0:T(8,128)S(1)} %shard_map.89), channel_id=1, replica_groups=mesh['z'=8,'x'=4,'y'=4,'c'=2] {'z','c'}, dimensions={0} | all-to-all | bytes 262144 | tf_op jit(solution)/shard_map/all_to_all | solution.py:171
  88.2 10.2 %all_to_all.32.residual_ref = f32[16,16,128]{2,1,0:T(8,128)S(1)} all-to-all(f32[16,16,128]{2,1,0:T(8,128)S(1)} %shard_map.90), channel_id=1, replica_groups=mesh['z'=8,'x'=4,'y'=4,'c'=2] {'x','y'}, dimensions={0} | all-to-all | bytes 262144 | tf_op jit(solution)/shard_map/all_to_all | solution.py:171
  98.4 0.0 copy-done.8
  98.4 0.0 copy-start.6
  98.4 0.9 copy-done.6
  99.4 0.4 shard_map.91
  99.8 9.8 %all_to_all.33.parts_ref = f32[16,16,128]{2,1,0:T(8,128)S(1)} all-to-all(f32[16,16,128]{2,1,0:T(8,128)S(1)} %shard_map.91), channel_id=1, replica_groups=mesh['z'=8,'x'=4,'y'=4,'c'=2] {'x','y'}, dimensions={0} | all-to-all | bytes 262144 | tf_op jit(solution)/shard_map/all_to_all | solution.py:171
  109.6 0.7 shard_map.92
  110.2 5.7 %all-to-all-start.5 = ((f32[16,16,128]{2,1,0:T(8,128)}), f32[16,16,128]{2,1,0:T(8,128)S(1)}, u32[]{:S(2)}, u32[]{:S(2)}) async-start(f32[16,16,128]{2,1,0:T(8,128)} %shard_map.92), calls=%async_computation.5 | async-start | bytes 262144 | tf_op jit(solution)/shard_map/all_to_all | solution.py:171
  116.0 0.1 constant_dynamic-slice_fusion
  116.0 0.7 copy.12
  116.7 8.4 %all-to-all-done.5.parts_ref = f32[16,16,128]{2,1,0:T(8,128)S(1)} async-done(((f32[16,16,128]{2,1,0:T(8,128)}), f32[16,16,128]{2,1,0:T(8,128)S(1)}, u32[]{:S(2)}, u32[]{:S(2)}) %all-to-all-start.5) | async-done | bytes 131104 | tf_op jit(solution)/shard_map/all_to_all | solution.py:171
  125.2 0.0 copy-done.11
  125.2 0.7 shard_map.93
  (6 shorter events, 0.1 us)
Async XLA Ops:
  0.6 41.7 %copy-start = (f32[16,8]{0,1:T(8,128)S(1)}, f32[16,8]{0,1:T(8,128)}, u32[]{:S(2)}) copy-start(f32[16,8]{0,1:T(8,128)} %param.9) | copy-start | bytes 1540
  0.7 1.6 %copy-start.1 = (bf16[4096,256]{1,0:T(8,128)(2,1)S(1)}, bf16[4096,256]{1,0:T(8,128)(2,1)}, u32[]{:S(2)}) copy-start(bf16[4096,256]{1,0:T(8,128)(2,1)} %centres_ref.5) | copy-start | bytes 6291460
  2.3 0.7 copy-start.9
  2.9 0.7 copy-start.10
  3.6 38.9 %copy-start.2 = (bf16[4096,256]{1,0:T(8,128)(2,1)S(1)}, bf16[4096,256]{1,0:T(8,128)(2,1)}, u32[]{:S(2)}) copy-start(bf16[4096,256]{1,0:T(8,128)(2,1)} %centres_ref.5) | copy-start | bytes 6291460
  3.6 38.9 %copy-start.4 = (f32[16,4096]{1,0:T(8,128)S(1)}, f32[16,4096]{1,0:T(8,128)}, u32[]{:S(2)}) copy-start(f32[16,4096]{1,0:T(8,128)} %weights_ref.1) | copy-start | bytes 786436
  39.3 5.8 %collective-permute-start = (bf16[8,16,8,256]{3,2,1,0:T(8,128)(2,1)S(1)}, bf16[8,16,8,256]{3,2,1,0:T(8,128)(2,1)S(1)}, u32[]{:S(2)}, u32[]{:S(2)}) collective-permute-start(bf16[8,16,8,256]{3,2,1,0:T(8,128)(2,1)S(1)} %bitcast.7), channel_id=1, source_target_pairs={{0,1},{1,0},{2,3},{3,2},{4,5},{5,4},{6,7},{7,6},{8,9},{9,8},{10,11... | collective-permute-start | bytes 1572872 | tf_op jit(solution)/shard_map/ppermute | solution.py:202
  43.7 1.3 %copy-start.3 = (f32[4096,128]{1,0:T(8,128)}, f32[4096,128]{1,0:T(8,128)S(1)}, u32[]{:S(2)}) copy-start(f32[4096,128]{1,0:T(8,128)S(1)} %get-tuple-element.12.norm_ref) | copy-start | bytes 6291460
  45.1 53.3 %copy-start.8 = (f32[64,128]{1,0:T(8,128)S(1)}, f32[64,128]{1,0:T(8,128)}, u32[]{:S(2)}) copy-start(f32[64,128]{1,0:T(8,128)} %vectors_ref.3) | copy-start | bytes 98308
  63.5 0.7 copy-start.5
  64.2 0.6 copy-start.7
  64.8 60.3 %copy-start.11 = (f32[128]{0:T(128)S(1)}, f32[128]{0:T(128)}, u32[]{:S(2)}) copy-start(f32[128]{0:T(128)} %param.13) | copy-start | bytes 1540
  64.8 10.4 %all-to-all-start.1 = ((f32[16,16,128]{2,1,0:T(8,128)}), f32[16,16,128]{2,1,0:T(8,128)S(1)}, u32[]{:S(2)}, u32[]{:S(2)}) async-start(f32[16,16,128]{2,1,0:T(8,128)} %copy-done.7), calls=%async_computation.1 | async-start | bytes 262144 | tf_op jit(solution)/shard_map/all_to_all | solution.py:171
  98.4 1.0 copy-start.6
  110.2 14.9 %all-to-all-start.5 = ((f32[16,16,128]{2,1,0:T(8,128)}), f32[16,16,128]{2,1,0:T(8,128)S(1)}, u32[]{:S(2)}, u32[]{:S(2)}) async-start(f32[16,16,128]{2,1,0:T(8,128)} %shard_map.92), calls=%async_computation.5 | async-start | bytes 262144 | tf_op jit(solution)/shard_map/all_to_all | solution.py:171

commit v2 on v1

v2 whole, which is shorter than its diff:
```python
import math

import jax
import jax.numpy as jnp
from jax import lax
from jax.experimental import pallas as pl
from jax.experimental.pallas import tpu as pltpu
from jax.sharding import Mesh
from jax.sharding import PartitionSpec as P

ALL = ("z", "x", "y", "c")
PLANE = ("x", "y")
COLUMN = ("z", "c")
CHUNK = 256
NT = (((1,), (1,)), ((), ()))
NN = (((1,), (0,)), ((), ()))
VMEM_LIMIT = 24 * 1024 * 1024


def split(v):
    hi = v.astype(jnp.bfloat16)
    lo = (v - hi.astype(jnp.float32)).astype(jnp.bfloat16)
    return hi, lo


def mxu(a, b, dims):
    return lax.dot_general(a, b, dims, preferred_element_type=jnp.float32)


def dot_f32(a, b, dims):
    rows = a.shape[0]
    both = jnp.concatenate(split(a), axis=0)
    b_hi, b_lo = split(b)
    out = mxu(both, b_hi, dims) + mxu(both, b_lo, dims)
    return out[:rows] + out[rows:]


def squares(v):
    wide = v.astype(jnp.float32)
    return split(wide * wide)


def pick_kernel(first_ref, batch_ref, centres_ref, rows_ref, index_ref, tiles_ref, index_sem, sems):
    own = batch_ref.shape[0]
    fetch = pltpu.make_async_copy(batch_ref, index_ref, index_sem)
    fetch.start()
    fetch.wait()
    first = first_ref[0]
    copies = []
    for r in range(own):
        row = index_ref[r] - first
        base = pl.multiple_of((row // 8) * 8, 8)
        copy = pltpu.make_async_copy(
            centres_ref.at[pl.ds(base, 8), :], tiles_ref.at[r], sems.at[r]
        )
        copy.start()
        copies.append(copy)
    sub = lax.broadcasted_iota(jnp.int32, tiles_ref.shape[1:], 0)
    picked = jnp.zeros(tiles_ref.shape[1:], jnp.float32)
    for r, copy in enumerate(copies):
        copy.wait()
        wanted = (index_ref[r] - first) % 8
        tile = jnp.where(sub == wanted, tiles_ref[r].astype(jnp.float32), 0.0)
        picked = jnp.where(sub == r, jnp.sum(tile, axis=0, keepdims=True), picked)
    rows_ref[...] = jnp.broadcast_to(picked.astype(jnp.bfloat16)[None], rows_ref.shape)


def prepare_kernel(
    first_ref, block_ref, centres_ref, weights_ref,
    norm_ref, points_ref, point_norm_ref, hi_ref, lo_ref, index_ref, index_sem,
):
    fetch = pltpu.make_async_copy(block_ref, index_ref, index_sem)
    fetch.start()
    ones = jnp.ones((centres_ref.shape[1], 128), jnp.bfloat16)

    def norms(v):
        hi, lo = squares(v)
        return mxu(hi, ones, NN) + mxu(lo, ones, NN)

    hi, lo = split(weights_ref[...])
    hi_ref[...] = hi
    lo_ref[...] = lo
    fetch.wait()
    first = first_ref[0]
    sub = lax.broadcasted_iota(jnp.int32, (8, 128), 0)
    lane = lax.broadcasted_iota(jnp.int32, (8, 128), 1)
    groups = []
    for start in range(0, points_ref.shape[0], 8):
        tile = jnp.zeros((8, 128), jnp.int32)
        for r in range(8):
            tile = jnp.where(sub == r, index_ref[start + r] - first, tile)
        groups.append(tile)
    found = jnp.zeros(points_ref.shape, jnp.float32)
    for base in range(0, centres_ref.shape[0], 256):
        centres = centres_ref[base : base + 256, :]
        norm_ref[base : base + 256, :] = norms(centres)
        pieces = []
        for tile in groups:
            halves = [jnp.where(tile == lane + (base + k), 1.0, 0.0) for k in (0, 128)]
            pieces.append(jnp.concatenate(halves, axis=1))
        hot = jnp.concatenate(pieces, axis=0).astype(jnp.bfloat16)
        found = found + mxu(hot, centres, NN)
    points = found.astype(jnp.bfloat16)
    points_ref[...] = points
    point_norm_ref[...] = norms(points)


def tile_kernel(
    core_ref, own_ref, other_ref, centres_ref, norm_ref, hi_ref, lo_ref, points_ref,
    point_norm_ref, out_ref, block_hi_ref, block_lo_ref,
):
    depth = centres_ref.shape[1]
    rows = jnp.concatenate([own_ref[0], other_ref[0], own_ref[1], other_ref[1]], axis=0)
    hi, lo = squares(rows)
    ones = jnp.ones((8, depth), jnp.bfloat16)
    row_norm = (mxu(ones, hi, NT) + mxu(ones, lo, NT))[:1]
    doubled = rows * jnp.bfloat16(-2.0)
    factor = -1.0 / (float(depth) ** 0.5 * math.log(2.0))

    def kernel_values(v, v_norm):
        wide = jnp.concatenate([v_norm, v_norm], axis=1)
        squared = jnp.maximum((wide + row_norm) + mxu(v, doubled, NT), 1.0)
        return jnp.exp2(squared * lax.rsqrt(squared) * factor)

    both_terms = jnp.concatenate([hi_ref[...], lo_ref[...]], axis=0)
    outputs = hi_ref.shape[0]
    total = jnp.zeros((2 * outputs, rows.shape[0]), jnp.float32)
    for base in range(0, centres_ref.shape[0], CHUNK):
        values = kernel_values(
            centres_ref[base : base + CHUNK, :], norm_ref[base : base + CHUNK, :]
        )
        k_hi = values.astype(jnp.bfloat16)
        rest = values - k_hi.astype(jnp.float32)
        terms = both_terms[:, base : base + CHUNK]
        total = total + mxu(terms, k_hi, NN)
        total = total + mxu(terms, rest.astype(jnp.bfloat16), NN)
    predicted = total[:outputs] + total[outputs:]
    block = kernel_values(points_ref[...], point_norm_ref[...])
    swapped = core_ref[0] == 1

    def ordered(v):
        return jnp.where(swapped, pltpu.roll(v, 64, 1), v)

    for h in range(2):
        out_ref[h] = ordered(predicted[:, h * 128 : (h + 1) * 128])
        b_hi, b_lo = split(ordered(block[:, h * 128 : (h + 1) * 128]))
        block_hi_ref[:, h * 128 : (h + 1) * 128] = b_hi
        block_lo_ref[:, h * 128 : (h + 1) * 128] = b_lo


def combine_kernel(parts_ref, less_ref, out_ref):
    total = jnp.sum(parts_ref[...], axis=0) - less_ref[...]
    out_ref[...] = jnp.broadcast_to(total[None], out_ref.shape)


def spread_kernel(parts_ref, out_ref):
    total = jnp.sum(parts_ref[...], axis=0)
    out_ref[...] = jnp.broadcast_to(total[None], out_ref.shape)


def project_kernel(residual_ref, block_hi_ref, block_lo_ref, vectors_ref, out_ref):
    residual = jnp.concatenate([residual_ref[h] for h in range(residual_ref.shape[0])], axis=1)
    rows = residual.shape[0]
    both = jnp.concatenate(split(residual), axis=0)
    along = mxu(both, block_hi_ref[...], NT) + mxu(both, block_lo_ref[...], NT)
    along = along[:rows] + along[rows:]
    projection = dot_f32(along, vectors_ref[...], NN)
    out_ref[...] = jnp.broadcast_to(projection[None], out_ref.shape)


def correct_kernel(parts_ref, scales_ref, vectors_ref, out_ref):
    projection = jnp.sum(parts_ref[...], axis=0) * scales_ref[...]
    out_ref[...] = dot_f32(projection, vectors_ref[...], NT)


def call(kernel, out, *args, **kwargs):
    return pl.pallas_call(
        kernel,
        out_shape=out,
        compiler_params=pltpu.CompilerParams(vmem_limit_bytes=VMEM_LIMIT),
        **kwargs,
    )(*args)


def shape(dims, dtype=jnp.float32):
    return jax.ShapeDtypeStruct(dims, dtype)


def local_part(first, core, centres, mine, other, weights, nystrom_index):
    count, depth = centres.shape
    plane, half, _ = mine.shape
    outputs = weights.shape[0]
    block = nystrom_index.shape[0]
    smem = pl.BlockSpec(memory_space=pltpu.SMEM)
    vmem = pl.BlockSpec(memory_space=pltpu.VMEM)
    anywhere = pl.BlockSpec(memory_space=pl.ANY)
    prepared = call(
        prepare_kernel,
        (
            shape((count, 128)),
            shape((block, depth), jnp.bfloat16),
            shape((block, 128)),
            shape((outputs, count), jnp.bfloat16),
            shape((outputs, count), jnp.bfloat16),
        ),
        first, nystrom_index, centres, weights,
        in_specs=[smem, anywhere, vmem, vmem],
        out_specs=(vmem,) * 5,
        scratch_shapes=[pltpu.SMEM((block,), jnp.int32), pltpu.SemaphoreType.DMA(())],
    )
    norm, points, point_norm, w_hi, w_lo = prepared
    rows_spec = pl.BlockSpec((2, half, depth), lambda i: (i, 0, 0))
    batch = plane * 128
    return call(
        tile_kernel,
        (
            shape((plane, outputs, 128)),
            shape((block, batch), jnp.bfloat16),
            shape((block, batch), jnp.bfloat16),
        ),
        core, mine, other, centres, norm, w_hi, w_lo, points, point_norm,
        grid=(plane // 2,),
        in_specs=[smem, rows_spec, rows_spec] + [vmem] * 6,
        out_specs=(
            pl.BlockSpec((2, outputs, 128), lambda i: (i, 0, 0)),
            pl.BlockSpec((block, 256), lambda i: (0, i)),
            pl.BlockSpec((block, 256), lambda i: (0, i)),
        ),
    )


def exchange(x, axes):
    return lax.all_to_all(x, axes, split_axis=0, concat_axis=0, tiled=True)


def on_device(centres, weights, targets, batch_index, nystrom_index, eigvecs, scales):
    count, depth = centres.shape
    outputs = weights.shape[0]
    own = batch_index.shape[0]
    block = nystrom_index.shape[0]
    anywhere = pl.BlockSpec(memory_space=pl.ANY)
    sizes = {a: lax.axis_size(a) for a in ALL}
    plane = sizes["x"] * sizes["y"]
    column = sizes["z"] * sizes["c"]
    first = (lax.axis_index(ALL) * count).astype(jnp.int32).reshape(1)
    core = lax.axis_index("c").astype(jnp.int32).reshape(1)
    place = lax.axis_index("c") * sizes["z"] + lax.axis_index("z")
    smem = pl.BlockSpec(memory_space=pltpu.SMEM)
    vmem = pl.BlockSpec(memory_space=pltpu.VMEM)

    rows = call(
        pick_kernel,
        shape((sizes["z"], own, depth), jnp.bfloat16),
        first, batch_index, centres,
        in_specs=[smem, anywhere, anywhere],
        out_specs=vmem,
        scratch_shapes=[
            pltpu.SMEM((own,), jnp.int32),
            pltpu.VMEM((own, 8, depth), jnp.bfloat16),
            pltpu.SemaphoreType.DMA(()),
            pltpu.SemaphoreType.DMA((own,)),
        ],
    )
    rows = exchange(rows, ("z",)).reshape(1, sizes["z"] * own, depth)
    mine = exchange(jnp.broadcast_to(rows, (plane, *rows.shape[1:])), PLANE)
    other = lax.ppermute(mine, "c", [(0, 1), (1, 0)])
    predicted, block_hi, block_lo = local_part(
        first, core, centres, mine, other, weights, nystrom_index
    )
    lanes = lax.broadcasted_iota(jnp.int32, (outputs, 128), 1) // own
    less = jnp.where(lanes == place, jnp.tile(targets, (1, 128 // own)), 0.0)
    gathered = exchange(predicted, PLANE)
    summed = call(combine_kernel, shape((column, outputs, 128)), gathered, less)
    summed = exchange(summed, COLUMN)
    residual = call(spread_kernel, shape((plane, outputs, 128)), summed)
    residual_local = lax.dynamic_slice(residual, (0, 0, place * own), (1, outputs, own))[0]
    residual = exchange(residual, PLANE)
    projection = call(
        project_kernel, shape((plane, outputs, 128)), residual, block_hi, block_lo, eigvecs
    )
    projection = exchange(projection, PLANE)
    projection = call(spread_kernel, shape((column, outputs, 128)), projection)
    projection = exchange(projection, COLUMN)
    correction = call(
        correct_kernel, shape((outputs, block)), projection, scales[None, :], eigvecs
    )
    return residual_local, correction


def solution(mesh):
    finer = Mesh(mesh.devices.reshape(mesh.shape["gx"], 4, 4, 2), ALL)
    in_specs = (
        P(ALL, None),
        P(None, ALL),
        P(None, ALL),
        P(ALL),
        P(ALL),
        P(ALL, None),
        P(),
    )
    out_specs = (P(None, ALL), P(None, ALL))
    return jax.shard_map(
        on_device, mesh=finer, in_specs=in_specs, out_specs=out_specs, check_vma=False
    )
```

time: 126 us -> 121 us (0.960)
  blocking collectives: 67.6 us -> 64.4 us
  local copies, waits for them, and re-layouts: 7.34 us -> 4.76 us
    all_to_all x4 -> x5, blocking collectives: 67.6 us -> 64.4 us  [exchange(): return lax.all_to_all(x, axes, split_axis=0, concat_axis=0, tiled=True)]
    unnamed x24 -> x20, local copies, waits for them, and re-layouts: 6.55 us -> 3.93 us
  transfers between devices with their start and end apart: 3 -> 3, of which waited for: 2 -> 2; matrix products, arithmetic and copies ran while one was open for 1% -> 1% of each run, Pallas kernels for 1% -> 2%
where the time goes in v2:
time: 121 us; the launch traced here: 120 us
  blocking collectives  64.4 us (53%)
  Pallas kernels  22.5 us (19%)
  waiting for transfers between devices  15.1 us (12%)
  starting transfers between devices  12.6 us (10%)
  local copies, waits for them, and re-layouts  4.76 us (4%)
    all_to_all x5, blocking collectives, exchange(): return lax.all_to_all(x, axes, split_axis=0, concat_axis=0, tiled=True)  64.4 us
    pallas_call x8, Pallas kernels, call(): pl.pallas_call(kernel, out_shape=out, compiler_params=pltpu.CompilerParam...  22.5 us
    all_to_all x2, waiting for transfers between devices, exchange(): return lax.all_to_all(x, axes, split_axis=0, concat_axis=0, tiled=True)  15.1 us
    all_to_all x2, starting transfers between devices, exchange(): return lax.all_to_all(x, axes, split_axis=0, concat_axis=0, tiled=True)  9.37 us
    unnamed x20, local copies, waits for them, and re-layouts  3.93 us
    ppermute x1, starting transfers between devices, on_device(): other = lax.ppermute(mine, 'c', [(0, 1), (1, 0)])  3.25 us
  transfers between devices with their start and end apart: 3, of which 2 were waited for; matrix products, arithmetic and copies ran while one was open for 1% of the time, Pallas kernels for 2%

profile of v2, /device:TPU:1, one launch (start us, length us, event | category | flops | bytes accessed | tf_op | source)
XLA Modules:
  0.0 120.2 jit_solution(12008745399410406498)
XLA Ops:
  0.6 0.0 copy-start
  0.6 0.0 copy-start.9
  0.7 0.0 copy-start.1
  0.7 1.6 %copy-done.1 = bf16[4096,256]{1,0:T(8,128)(2,1)S(1)} copy-done((bf16[4096,256]{1,0:T(8,128)(2,1)S(1)}, bf16[4096,256]{1,0:T(8,128)(2,1)}, u32[]{:S(2)}) %copy-start.1) | copy-done | bytes 2097176
  2.3 0.0 copy-start.8
  2.3 0.7 copy-done.8
  2.9 0.0 copy-start.2
  2.9 0.0 copy-start.3
  2.9 0.9 shard_map.86
  3.8 15.7 %all_to_all.35 = bf16[8,8,256]{2,1,0:T(8,128)(2,1)S(1)} all-to-all(bf16[8,8,256]{2,1,0:T(8,128)(2,1)S(1)} %shard_map.86), channel_id=1, replica_groups=mesh['z'=8,'x'=4,'y'=4,'c'=2] {'z'}, dimensions={0} | all-to-all | bytes 65536 | tf_op jit(solution)/shard_map/all_to_all | solution.py:233
  19.5 15.8 %all_to_all.36.own_ref = bf16[16,64,256]{2,1,0:T(8,128)(2,1)S(1)} all-to-all(bf16[16,64,256]{2,1,0:T(8,128)(2,1)S(1)} %broadcast_in_dim.15), channel_id=1, replica_groups=mesh['z'=8,'x'=4,'y'=4,'c'=2] {'x','y'}, dimensions={0} | all-to-all | bytes 1048576 | tf_op jit(solution)/shard_map/all_to_all | solution.py:233
  35.3 3.2 %collective-permute-start = (bf16[16,64,256]{2,1,0:T(8,128)(2,1)S(1)}, bf16[16,64,256]{2,1,0:T(8,128)(2,1)S(1)}, u32[]{:S(2)}, u32[]{:S(2)}) collective-permute-start(bf16[16,64,256]{2,1,0:T(8,128)(2,1)S(1)} %all_to_all.36.own_ref), channel_id=1, source_target_pairs={{0,1},{1,0},{2,3},{3,2},{4,5},{5,4},{6,7},{7,6},{8,9},{9,8},{10,11... | collective-permute-start | bytes 1572872 | tf_op jit(solution)/shard_map/ppermute | solution.py:266
  38.6 0.0 copy-done
  38.6 0.1 copy.11
  38.6 0.0 copy-done.9
  38.6 0.0 copy-done.2
  38.6 0.0 copy-done.3
  38.6 2.2 %shard_map.87 = (f32[4096,128]{1,0:T(8,128)S(1)}, bf16[64,256]{1,0:T(8,128)(2,1)S(1)}, f32[64,128]{1,0:T(8,128)S(1)}, bf16[16,4096]{1,0:T(8,128)(2,1)S(1)}, bf16[16,4096]{1,0:T(8,128)(2,1)S(1)}) custom-call(s32[1]{0:T(128)} %bitcast.1.first_ref, s32[64]{0:T(128)S(1)} %copy-done.9, bf16[4096,256]{1,0:T(8,128)(2,1)S(1)} %copy-done.2, f32[16,4096]{1,0:T(8,128)S(1)} %copy-done.3), custom_call_target="tpu_custom_call" | custom-call | tf_op jit(solution)/shard_map/pallas_call | solution.py:177
  40.8 0.0 collective-permute-done.other_ref
  40.8 0.0 copy-start.6
  40.9 17.6 %shard_map.88 = (f32[16,16,128]{2,1,0:T(8,128)}, bf16[64,2048]{1,0:T(8,128)(2,1)S(1)}, bf16[64,2048]{1,0:T(8,128)(2,1)S(1)}) custom-call(s32[1]{0:T(128)} %bitcast.core_ref, bf16[16,64,256]{2,1,0:T(8,128)(2,1)S(1)} %all_to_all.36.own_ref, bf16[16,64,256]{2,1,0:T(8,128)(2,1)S(1)} %collective-permute-done.other_ref, bf16[4096,256]{1,0:T(8,128)(2,1)S(1)} %copy-done.2, ...), custom_call_target="tpu_custom_call" | custom-call | tf_op jit(solution)/shard_map/pallas_call | solution.py:177
  58.5 0.0 copy-start.4
  58.5 0.7 copy-done.4
  59.2 0.0 copy-start.7
  59.2 3.6 %all-to-all-start.2 = ((f32[16,16,128]{2,1,0:T(8,128)}), f32[16,16,128]{2,1,0:T(8,128)S(1)}, u32[]{:S(2)}, u32[]{:S(2)}) async-start(f32[16,16,128]{2,1,0:T(8,128)} %get-tuple-element.15), calls=%async_computation.2 | async-start | bytes 262144 | tf_op jit(solution)/shard_map/all_to_all | solution.py:233
  62.8 6.7 %all-to-all-done.2.parts_ref = f32[16,16,128]{2,1,0:T(8,128)S(1)} async-done(((f32[16,16,128]{2,1,0:T(8,128)}), f32[16,16,128]{2,1,0:T(8,128)S(1)}, u32[]{:S(2)}, u32[]{:S(2)}) %all-to-all-start.2) | async-done | bytes 131104 | tf_op jit(solution)/shard_map/all_to_all | solution.py:233
  69.5 12.9 %all_to_all.37.parts_ref = f32[16,16,128]{2,1,0:T(8,128)S(1)} all-to-all(f32[16,16,128]{2,1,0:T(8,128)S(1)} %shard_map.89), channel_id=1, replica_groups=mesh['z'=8,'x'=4,'y'=4,'c'=2] {'z','c'}, dimensions={0} | all-to-all | bytes 262144 | tf_op jit(solution)/shard_map/all_to_all | solution.py:233
  82.5 10.2 %all_to_all.38.residual_ref = f32[16,16,128]{2,1,0:T(8,128)S(1)} all-to-all(f32[16,16,128]{2,1,0:T(8,128)S(1)} %shard_map.90), channel_id=1, replica_groups=mesh['z'=8,'x'=4,'y'=4,'c'=2] {'x','y'}, dimensions={0} | all-to-all | bytes 262144 | tf_op jit(solution)/shard_map/all_to_all | solution.py:233
  92.7 0.0 copy-done.6
  92.7 0.0 copy-start.5
  92.7 0.9 copy-done.5
  93.7 0.4 shard_map.91
  94.1 9.8 %all_to_all.39.parts_ref = f32[16,16,128]{2,1,0:T(8,128)S(1)} all-to-all(f32[16,16,128]{2,1,0:T(8,128)S(1)} %shard_map.91), channel_id=1, replica_groups=mesh['z'=8,'x'=4,'y'=4,'c'=2] {'x','y'}, dimensions={0} | all-to-all | bytes 262144 | tf_op jit(solution)/shard_map/all_to_all | solution.py:233
  103.9 0.7 shard_map.92
  104.6 5.7 %all-to-all-start.6 = ((f32[16,16,128]{2,1,0:T(8,128)}), f32[16,16,128]{2,1,0:T(8,128)S(1)}, u32[]{:S(2)}, u32[]{:S(2)}) async-start(f32[16,16,128]{2,1,0:T(8,128)} %shard_map.92), calls=%async_computation.6 | async-start | bytes 262144 | tf_op jit(solution)/shard_map/all_to_all | solution.py:233
  110.3 0.1 constant_dynamic-slice_fusion
  110.4 0.7 copy.12
  111.0 8.4 %all-to-all-done.6.parts_ref = f32[16,16,128]{2,1,0:T(8,128)S(1)} async-done(((f32[16,16,128]{2,1,0:T(8,128)}), f32[16,16,128]{2,1,0:T(8,128)S(1)}, u32[]{:S(2)}, u32[]{:S(2)}) %all-to-all-start.6) | async-done | bytes 131104 | tf_op jit(solution)/shard_map/all_to_all | solution.py:233
  119.5 0.0 copy-done.7
  119.5 0.7 shard_map.93
  (7 shorter events, 0.1 us)
Async XLA Ops:
  0.6 37.9 %copy-start = (f32[16,8]{0,1:T(8,128)S(1)}, f32[16,8]{0,1:T(8,128)}, u32[]{:S(2)}) copy-start(f32[16,8]{0,1:T(8,128)} %param.9) | copy-start | bytes 1540
  0.6 38.0 %copy-start.9 = (s32[64]{0:T(128)S(1)}, s32[64]{0:T(128)}, u32[]{:S(2)}) copy-start(s32[64]{0:T(128)} %block_ref.1) | copy-start | bytes 772
  0.7 1.6 %copy-start.1 = (bf16[4096,256]{1,0:T(8,128)(2,1)S(1)}, bf16[4096,256]{1,0:T(8,128)(2,1)}, u32[]{:S(2)}) copy-start(bf16[4096,256]{1,0:T(8,128)(2,1)} %centres_ref.5) | copy-start | bytes 6291460
  2.3 0.7 copy-start.8
  2.9 35.7 %copy-start.2 = (bf16[4096,256]{1,0:T(8,128)(2,1)S(1)}, bf16[4096,256]{1,0:T(8,128)(2,1)}, u32[]{:S(2)}) copy-start(bf16[4096,256]{1,0:T(8,128)(2,1)} %centres_ref.5) | copy-start | bytes 6291460
  2.9 35.7 %copy-start.3 = (f32[16,4096]{1,0:T(8,128)S(1)}, f32[16,4096]{1,0:T(8,128)}, u32[]{:S(2)}) copy-start(f32[16,4096]{1,0:T(8,128)} %weights_ref.1) | copy-start | bytes 786436
  35.3 5.5 %collective-permute-start = (bf16[16,64,256]{2,1,0:T(8,128)(2,1)S(1)}, bf16[16,64,256]{2,1,0:T(8,128)(2,1)S(1)}, u32[]{:S(2)}, u32[]{:S(2)}) collective-permute-start(bf16[16,64,256]{2,1,0:T(8,128)(2,1)S(1)} %all_to_all.36.own_ref), channel_id=1, source_target_pairs={{0,1},{1,0},{2,3},{3,2},{4,5},{5,4},{6,7},{7,6},{8,9},{9,8},{10,11... | collective-permute-start | bytes 1572872 | tf_op jit(solution)/shard_map/ppermute | solution.py:266
  40.8 51.9 %copy-start.6 = (f32[64,128]{1,0:T(8,128)S(1)}, f32[64,128]{1,0:T(8,128)}, u32[]{:S(2)}) copy-start(f32[64,128]{1,0:T(8,128)} %vectors_ref.3) | copy-start | bytes 98308
  58.5 0.7 copy-start.4
  59.2 60.3 %copy-start.7 = (f32[128]{0:T(128)S(1)}, f32[128]{0:T(128)}, u32[]{:S(2)}) copy-start(f32[128]{0:T(128)} %param.13) | copy-start | bytes 1540
  59.2 10.4 %all-to-all-start.2 = ((f32[16,16,128]{2,1,0:T(8,128)}), f32[16,16,128]{2,1,0:T(8,128)S(1)}, u32[]{:S(2)}, u32[]{:S(2)}) async-start(f32[16,16,128]{2,1,0:T(8,128)} %get-tuple-element.15), calls=%async_computation.2 | async-start | bytes 262144 | tf_op jit(solution)/shard_map/all_to_all | solution.py:233
  92.7 1.0 copy-start.5
  104.6 14.9 %all-to-all-start.6 = ((f32[16,16,128]{2,1,0:T(8,128)}), f32[16,16,128]{2,1,0:T(8,128)S(1)}, u32[]{:S(2)}, u32[]{:S(2)}) async-start(f32[16,16,128]{2,1,0:T(8,128)} %shard_map.92), calls=%async_computation.6 | async-start | bytes 262144 | tf_op jit(solution)/shard_map/all_to_all | solution.py:233

commit v3 on v2

--- a/solution.py
+++ b/solution.py
@@ -7,6 +7,7 @@
 from jax.experimental.pallas import tpu as pltpu
 from jax.sharding import Mesh
 from jax.sharding import PartitionSpec as P
+
 
 ALL = ("z", "x", "y", "c")
 PLANE = ("x", "y")
@@ -65,21 +66,17 @@
     rows_ref[...] = jnp.broadcast_to(picked.astype(jnp.bfloat16)[None], rows_ref.shape)
 
 
-def prepare_kernel(
-    first_ref, block_ref, centres_ref, weights_ref,
-    norm_ref, points_ref, point_norm_ref, hi_ref, lo_ref, index_ref, index_sem,
+def norms(v):
+    ones = jnp.ones((v.shape[1], 128), jnp.bfloat16)
+    hi, lo = squares(v)
+    return mxu(hi, ones, NN) + mxu(lo, ones, NN)
+
+
+def points_kernel(
+    first_ref, block_ref, centres_ref, points_ref, point_norm_ref, index_ref, index_sem
 ):
     fetch = pltpu.make_async_copy(block_ref, index_ref, index_sem)
     fetch.start()
-    ones = jnp.ones((centres_ref.shape[1], 128), jnp.bfloat16)
-
-    def norms(v):
-        hi, lo = squares(v)
-        return mxu(hi, ones, NN) + mxu(lo, ones, NN)
-
-    hi, lo = split(weights_ref[...])
-    hi_ref[...] = hi
-    lo_ref[...] = lo
     fetch.wait()
     first = first_ref[0]
     sub = lax.broadcasted_iota(jnp.int32, (8, 128), 0)
@@ -92,25 +89,28 @@
         groups.append(tile)
     found = jnp.zeros(points_ref.shape, jnp.float32)
     for base in range(0, centres_ref.shape[0], 256):
-        centres = centres_ref[base : base + 256, :]
-        norm_ref[base : base + 256, :] = norms(centres)
         pieces = []
         for tile in groups:
             halves = [jnp.where(tile == lane + (base + k), 1.0, 0.0) for k in (0, 128)]
             pieces.append(jnp.concatenate(halves, axis=1))
         hot = jnp.concatenate(pieces, axis=0).astype(jnp.bfloat16)
-        found = found + mxu(hot, centres, NN)
+        found = found + mxu(hot, centres_ref[base : base + 256, :], NN)
     points = found.astype(jnp.bfloat16)
     points_ref[...] = points
     point_norm_ref[...] = norms(points)
 
 
-def tile_kernel(
-    core_ref, own_ref, other_ref, centres_ref, norm_ref, hi_ref, lo_ref, points_ref,
-    point_norm_ref, out_ref, block_hi_ref, block_lo_ref,
-):
-    depth = centres_ref.shape[1]
-    rows = jnp.concatenate([own_ref[0], other_ref[0], own_ref[1], other_ref[1]], axis=0)
+def norm_kernel(centres_ref, weights_ref, norm_ref, hi_ref, lo_ref):
+    for base in range(0, centres_ref.shape[0], 256):
+        norm_ref[base : base + 256, :] = norms(centres_ref[base : base + 256, :])
+    hi, lo = split(weights_ref[...])
+    hi_ref[...] = hi
+    lo_ref[...] = lo
+
+
+def kernel_of(own_ref, other_ref, spans):
+    rows = jnp.concatenate([ref[h] for h in spans for ref in (own_ref, other_ref)], axis=0)
+    depth = rows.shape[1]
     hi, lo = squares(rows)
     ones = jnp.ones((8, depth), jnp.bfloat16)
     row_norm = (mxu(ones, hi, NT) + mxu(ones, lo, NT))[:1]
@@ -118,13 +118,37 @@
     factor = -1.0 / (float(depth) ** 0.5 * math.log(2.0))
 
     def kernel_values(v, v_norm):
-        wide = jnp.concatenate([v_norm, v_norm], axis=1)
+        wide = jnp.concatenate([v_norm] * (rows.shape[0] // 128), axis=1)
         squared = jnp.maximum((wide + row_norm) + mxu(v, doubled, NT), 1.0)
         return jnp.exp2(squared * lax.rsqrt(squared) * factor)
 
+    return kernel_values
+
+
+def ordered(v, core):
+    return jnp.where(core == 1, pltpu.roll(v, 64, 1), v)
+
+
+def mixed_kernel(
+    core_ref, own_ref, other_ref, points_ref, point_norm_ref, vectors_ref, out_ref
+):
+    e_hi, e_lo = split(vectors_ref[...].T)
+    left = jnp.concatenate([e_hi, e_lo, e_hi], axis=1)
+    for h in range(0, own_ref.shape[0], 2):
+        block = kernel_of(own_ref, other_ref, range(h, h + 2))(points_ref[...], point_norm_ref[...])
+        b_hi, b_lo = split(block)
+        mixed = mxu(left, jnp.concatenate([b_hi, b_hi, b_lo], axis=0), NN)
+        for k in range(2):
+            out_ref[h + k] = ordered(mixed[:, k * 128 : (k + 1) * 128], core_ref[0])
+
+
+def tile_kernel(
+    core_ref, own_ref, other_ref, centres_ref, norm_ref, hi_ref, lo_ref, out_ref,
+):
+    kernel_values = kernel_of(own_ref, other_ref, range(2))
     both_terms = jnp.concatenate([hi_ref[...], lo_ref[...]], axis=0)
     outputs = hi_ref.shape[0]
-    total = jnp.zeros((2 * outputs, rows.shape[0]), jnp.float32)
+    total = jnp.zeros((2 * outputs, 4 * own_ref.shape[1]), jnp.float32)
     for base in range(0, centres_ref.shape[0], CHUNK):
         values = kernel_values(
             centres_ref[base : base + CHUNK, :], norm_ref[base : base + CHUNK, :]
@@ -135,17 +159,8 @@
         total = total + mxu(terms, k_hi, NN)
         total = total + mxu(terms, rest.astype(jnp.bfloat16), NN)
     predicted = total[:outputs] + total[outputs:]
-    block = kernel_values(points_ref[...], point_norm_ref[...])
-    swapped = core_ref[0] == 1
-
-    def ordered(v):
-        return jnp.where(swapped, pltpu.roll(v, 64, 1), v)
-
     for h in range(2):
-        out_ref[h] = ordered(predicted[:, h * 128 : (h + 1) * 128])
-        b_hi, b_lo = split(ordered(block[:, h * 128 : (h + 1) * 128]))
-        block_hi_ref[:, h * 128 : (h + 1) * 128] = b_hi
-        block_lo_ref[:, h * 128 : (h + 1) * 128] = b_lo
+        out_ref[h] = ordered(predicted[:, h * 128 : (h + 1) * 128], core_ref[0])
 
 
 def combine_kernel(parts_ref, less_ref, out_ref):
@@ -158,13 +173,10 @@
     out_ref[...] = jnp.broadcast_to(total[None], out_ref.shape)
 
 
-def project_kernel(residual_ref, block_hi_ref, block_lo_ref, vectors_ref, out_ref):
-    residual = jnp.concatenate([residual_ref[h] for h in range(residual_ref.shape[0])], axis=1)
-    rows = residual.shape[0]
-    both = jnp.concatenate(split(residual), axis=0)
-    along = mxu(both, block_hi_ref[...], NT) + mxu(both, block_lo_ref[...], NT)
-    along = along[:rows] + along[rows:]
-    projection = dot_f32(along, vectors_ref[...], NN)
+def project_kernel(parts_ref, mixed_ref, residual_ref, out_ref):
+    residual = jnp.sum(parts_ref[...], axis=0)
+    residual_ref[...] = residual
+    projection = dot_f32(residual, jnp.sum(mixed_ref[...], axis=0), NT)
     out_ref[...] = jnp.broadcast_to(projection[None], out_ref.shape)
 
 
@@ -186,47 +198,59 @@
     return jax.ShapeDtypeStruct(dims, dtype)
 
 
-def local_part(first, core, centres, mine, other, weights, nystrom_index):
+def local_part(first, core, centres, mine, other, weights, nystrom_index, eigvecs, move):
     count, depth = centres.shape
     plane, half, _ = mine.shape
     outputs = weights.shape[0]
     block = nystrom_index.shape[0]
+    eigen = eigvecs.shape[1]
     smem = pl.BlockSpec(memory_space=pltpu.SMEM)
     vmem = pl.BlockSpec(memory_space=pltpu.VMEM)
-    anywhere = pl.BlockSpec(memory_space=pl.ANY)
-    prepared = call(
-        prepare_kernel,
+    stay = pl.BlockSpec(memory_space=pltpu.HBM)
+    points, point_norm = call(
+        points_kernel,
+        (shape((block, depth), jnp.bfloat16), shape((block, 128))),
+        first, keep(nystrom_index), centres,
+        in_specs=[smem, stay, vmem],
+        out_specs=(vmem,) * 2,
+        scratch_shapes=[pltpu.SMEM((block,), jnp.int32), pltpu.SemaphoreType.DMA(())],
+    )
+    mixed = call(
+        mixed_kernel, shape((plane, eigen, 128)),
+        core, mine, other, points, point_norm, eigvecs,
+        in_specs=[smem] + [vmem] * 5,
+        out_specs=vmem,
+    )
+    mixed = move(mixed)
+    norm, w_hi, w_lo = call(
+        norm_kernel,
         (
             shape((count, 128)),
-            shape((block, depth), jnp.bfloat16),
-            shape((block, 128)),
             shape((outputs, count), jnp.bfloat16),
             shape((outputs, count), jnp.bfloat16),
         ),
-        first, nystrom_index, centres, weights,
-        in_specs=[smem, anywhere, vmem, vmem],
-        out_specs=(vmem,) * 5,
-        scratch_shapes=[pltpu.SMEM((block,), jnp.int32), pltpu.SemaphoreType.DMA(())],
-    )
-    norm, points, point_norm, w_hi, w_lo = prepared
+        centres, weights,
+        in_specs=[vmem] * 2,
+        out_specs=(vmem,) * 3,
+    )
     rows_spec = pl.BlockSpec((2, half, depth), lambda i: (i, 0, 0))
-    batch = plane * 128
-    return call(
-        tile_kernel,
-        (
-            shape((plane, outputs, 128)),
-            shape((block, batch), jnp.bfloat16),
-            shape((block, batch), jnp.bfloat16),
+    predicted = call(
+        tile_kernel, shape((plane, outputs, 128)),
+        core, mine, other, centres, norm, w_hi, w_lo,
+        grid=(plane // 2,),
+        in_specs=[smem, rows_spec, rows_spec] + [vmem] * 4,
+        out_specs=pl.BlockSpec((2, outputs, 128), lambda i: (i, 0, 0)),
+        cost_estimate=pl.CostEstimate(
+            flops=3 * 2 * count * 2 * plane * half * depth,
+            transcendentals=2 * count * 2 * plane * half,
+            bytes_accessed=8 * count * depth,
         ),
-        core, mine, other, centres, norm, w_hi, w_lo, points, point_norm,
-        grid=(plane // 2,),
-        in_specs=[smem, rows_spec, rows_spec] + [vmem] * 6,
-        out_specs=(
-            pl.BlockSpec((2, outputs, 128), lambda i: (i, 0, 0)),
-            pl.BlockSpec((block, 256), lambda i: (0, i)),
-            pl.BlockSpec((block, 256), lambda i: (0, i)),
-        ),
-    )
+    )
+    return lax.optimization_barrier((predicted, mixed))
+
+
+def keep(x):
+    return pltpu.with_memory_space_constraint(x, pltpu.HBM)
 
 
 def exchange(x, axes):
@@ -238,7 +262,7 @@
     outputs = weights.shape[0]
     own = batch_index.shape[0]
     block = nystrom_index.shape[0]
-    anywhere = pl.BlockSpec(memory_space=pl.ANY)
+    stay = pl.BlockSpec(memory_space=pltpu.HBM)
     sizes = {a: lax.axis_size(a) for a in ALL}
     plane = sizes["x"] * sizes["y"]
     column = sizes["z"] * sizes["c"]
@@ -251,8 +275,8 @@
     rows = call(
         pick_kernel,
         shape((sizes["z"], own, depth), jnp.bfloat16),
-        first, batch_index, centres,
-        in_specs=[smem, anywhere, anywhere],
+        first, keep(batch_index), keep(centres),
+        in_specs=[smem, stay, stay],
         out_specs=vmem,
         scratch_shapes=[
             pltpu.SMEM((own,), jnp.int32),
@@ -264,20 +288,21 @@
     rows = exchange(rows, ("z",)).reshape(1, sizes["z"] * own, depth)
     mine = exchange(jnp.broadcast_to(rows, (plane, *rows.shape[1:])), PLANE)
     other = lax.ppermute(mine, "c", [(0, 1), (1, 0)])
-    predicted, block_hi, block_lo = local_part(
-        first, core, centres, mine, other, weights, nystrom_index
+    predicted, mixed = local_part(
+        first, core, centres, mine, other, weights, nystrom_index, eigvecs,
+        lambda v: exchange(v, PLANE),
     )
     lanes = lax.broadcasted_iota(jnp.int32, (outputs, 128), 1) // own
     less = jnp.where(lanes == place, jnp.tile(targets, (1, 128 // own)), 0.0)
     gathered = exchange(predicted, PLANE)
     summed = call(combine_kernel, shape((column, outputs, 128)), gathered, less)
     summed = exchange(summed, COLUMN)
-    residual = call(spread_kernel, shape((plane, outputs, 128)), summed)
-    residual_local = lax.dynamic_slice(residual, (0, 0, place * own), (1, outputs, own))[0]
-    residual = exchange(residual, PLANE)
-    projection = call(
-        project_kernel, shape((plane, outputs, 128)), residual, block_hi, block_lo, eigvecs
-    )
+    residual, projection = call(
+        project_kernel,
+        (shape((outputs, 128)), shape((plane, outputs, 128))),
+        summed, mixed,
+    )
+    residual_local = lax.dynamic_slice(residual, (0, place * own), (outputs, own))
     projection = exchange(projection, PLANE)
     projection = call(spread_kernel, shape((column, outputs, 128)), projection)
     projection = exchange(projection, COLUMN)

time: 121 us -> 124 us (1.025)
  blocking collectives: 64.4 us -> 55 us
  starting transfers between devices: 12.6 us -> 18 us
  Pallas kernels: 22.5 us -> 26.6 us
  local copies, waits for them, and re-layouts: 4.76 us -> 8.08 us
    all_to_all x5 -> x4, blocking collectives: 64.4 us -> 55 us  [exchange(): return lax.all_to_all(x, axes, split_axis=0, concat_axis=0, tiled=True)]
    all_to_all x2 -> x3, starting transfers between devices: 9.37 us -> 14.7 us  [exchange(): return lax.all_to_all(x, axes, split_axis=0, concat_axis=0, tiled=True)]
    pallas_call x8 -> x9, Pallas kernels: 22.5 us -> 26.6 us  [call(): pl.pallas_call(kernel, out_shape=out, compiler_params=pltpu.CompilerParam...]
    unnamed x20 -> x31, local copies, waits for them, and re-layouts: 3.93 us -> 7.91 us
    all_to_all x2 -> x3, waiting for transfers between devices: 15.1 us -> 15.1 us  [exchange(): return lax.all_to_all(x, axes, split_axis=0, concat_axis=0, tiled=True)]
  transfers between devices with their start and end apart: 3 -> 4, of which waited for: 2 -> 2; matrix products, arithmetic and copies ran while one was open for 1% -> 1% of each run, Pallas kernels for 2% -> 16%
where the time goes in v3:
time: 124 us
  blocking collectives  55 us (44%)
  Pallas kernels  26.6 us (21%)
  starting transfers between devices  18 us (15%)
  waiting for transfers between devices  15.1 us (12%)
  local copies, waits for them, and re-layouts  8.08 us (7%)
    all_to_all x4, blocking collectives, exchange(): return lax.all_to_all(x, axes, split_axis=0, concat_axis=0, tiled=True)  55 us
    pallas_call x9, Pallas kernels, call(): pl.pallas_call(kernel, out_shape=out, compiler_params=pltpu.CompilerParam...  26.6 us
    all_to_all x3, waiting for transfers between devices, exchange(): return lax.all_to_all(x, axes, split_axis=0, concat_axis=0, tiled=True)  15.1 us
    all_to_all x3, starting transfers between devices, exchange(): return lax.all_to_all(x, axes, split_axis=0, concat_axis=0, tiled=True)  14.7 us
    unnamed x31, local copies, waits for them, and re-layouts  7.91 us
    ppermute x1, starting transfers between devices, on_device(): other = lax.ppermute(mine, 'c', [(0, 1), (1, 0)])  3.25 us
  transfers between devices with their start and end apart: 4, of which 2 were waited for; matrix products, arithmetic and copies ran while one was open for 1% of the time, Pallas kernels for 16%

profile of v3, /device:TPU:1, one launch (start us, length us, event | category | flops | bytes accessed | tf_op | source)
XLA Modules:
  0.0 123.7 jit_solution(11654412039923643824)
XLA Ops:
  0.6 0.0 copy-start
  0.6 0.0 copy-start.1
  0.7 0.0 copy-start.6
  0.7 1.7 %shard_map.86 = bf16[8,8,256]{2,1,0:T(8,128)(2,1)S(1)} custom-call(s32[1]{0:T(128)} %bitcast.1.first_ref, s32[8]{0:T(128)} %batch_ref.1, bf16[4096,256]{1,0:T(8,128)(2,1)} %centres_ref.7), custom_call_target="tpu_custom_call" | custom-call | tf_op jit(solution)/shard_map/pallas_call | solution.py:189
  2.4 15.7 %all_to_all.35 = bf16[8,8,256]{2,1,0:T(8,128)(2,1)S(1)} all-to-all(bf16[8,8,256]{2,1,0:T(8,128)(2,1)S(1)} %shard_map.86), channel_id=1, replica_groups=mesh['z'=8,'x'=4,'y'=4,'c'=2] {'z'}, dimensions={0} | all-to-all | bytes 65536 | tf_op jit(solution)/shard_map/all_to_all | solution.py:257
  18.1 15.8 %all_to_all.36.own_ref = bf16[16,64,256]{2,1,0:T(8,128)(2,1)S(1)} all-to-all(bf16[16,64,256]{2,1,0:T(8,128)(2,1)S(1)} %broadcast_in_dim.15), channel_id=1, replica_groups=mesh['z'=8,'x'=4,'y'=4,'c'=2] {'x','y'}, dimensions={0} | all-to-all | bytes 1048576 | tf_op jit(solution)/shard_map/all_to_all | solution.py:257
  33.9 0.0 copy-start.2
  33.9 3.2 %collective-permute-start = (bf16[16,64,256]{2,1,0:T(8,128)(2,1)S(1)}, bf16[16,64,256]{2,1,0:T(8,128)(2,1)S(1)}, u32[]{:S(2)}, u32[]{:S(2)}) collective-permute-start(bf16[16,64,256]{2,1,0:T(8,128)(2,1)S(1)} %all_to_all.36.own_ref), channel_id=1, source_target_pairs={{0,1},{1,0},{2,3},{3,2},{4,5},{5,4},{6,7},{7,6},{8,9},{9,8},{10,11... | collective-permute-start | bytes 1572872 | tf_op jit(solution)/shard_map/ppermute | solution.py:290
  37.1 0.0 copy-done.1
  37.2 0.0 copy-done.6
  37.2 0.0 copy-start.7
  37.2 1.3 %shard_map.87 = (f32[4096,128]{1,0:T(8,128)S(1)}, bf16[16,4096]{1,0:T(8,128)(2,1)S(1)}, bf16[16,4096]{1,0:T(8,128)(2,1)S(1)}) custom-call(bf16[4096,256]{1,0:T(8,128)(2,1)S(1)} %copy-done.1, f32[16,4096]{1,0:T(8,128)S(1)} %copy-done.6), custom_call_target="tpu_custom_call" | custom-call | tf_op jit(solution)/shard_map/pallas_call | solution.py:189
  38.4 0.0 copy-start.9
  38.4 1.3 %copy-done.9 = f32[4096,128]{1,0:T(8,128)} copy-done((f32[4096,128]{1,0:T(8,128)}, f32[4096,128]{1,0:T(8,128)S(1)}, u32[]{:S(2)}) %copy-start.9) | copy-done | bytes 2097176
  39.8 0.0 copy-start.11
  39.8 0.7 copy-done.11
  40.4 0.0 copy-start.13
  40.4 0.7 copy-done.13
  41.1 1.3 %shard_map.89 = (bf16[64,256]{1,0:T(8,128)(2,1)S(1)}, f32[64,128]{1,0:T(8,128)S(1)}) custom-call(s32[1]{0:T(128)} %bitcast.1.first_ref, s32[64]{0:T(128)} %block_ref.1, bf16[4096,256]{1,0:T(8,128)(2,1)S(1)} %copy-done.1), custom_call_target="tpu_custom_call" | custom-call | tf_op jit(solution)/shard_map/pallas_call | solution.py:189
  42.4 0.0 copy-done
  42.4 0.1 copy.11
  42.5 0.0 collective-permute-done.other_ref
  42.5 0.0 copy-start.4
  42.5 0.0 copy-done.2
  42.5 0.0 copy-done.7
  42.5 0.0 copy-start.12
  42.6 3.6 %shard_map.90 = f32[16,128,128]{2,1,0:T(8,128)} custom-call(s32[1]{0:T(128)} %bitcast.core_ref, bf16[16,64,256]{2,1,0:T(8,128)(2,1)S(1)} %all_to_all.36.own_ref, bf16[16,64,256]{2,1,0:T(8,128)(2,1)S(1)} %collective-permute-done.other_ref, bf16[64,256]{1,0:T(8,128)(2,1)S(1)} %get-tuple-element.14.points_ref, f32[64,128]{1,0:T(8,128)S(1)} %get-tuple-element.15.point_norm_ref, ...), custom_call_target="tpu_custom_call" | custom-call | tf_op jit(solution)/shard_map/pallas_call | solution.py:189
  46.2 0.0 copy-done.4
  46.2 3.7 %all-to-all-start.2 = ((f32[16,128,128]{2,1,0:T(8,128)}), f32[16,128,128]{2,1,0:T(8,128)S(1)}, u32[]{:S(2)}, u32[]{:S(2)}) async-start(f32[16,128,128]{2,1,0:T(8,128)} %shard_map.90), calls=%async_computation.2 | async-start | bytes 2097152 | tf_op jit(solution)/shard_map/all_to_all | solution.py:257
  49.9 0.0 copy-done.12
  49.9 0.0 copy-start.3
  49.9 1.0 copy-done.3
  50.9 0.0 copy-start.5
  50.9 1.0 copy-done.5
  51.9 0.0 copy-start.10
  52.0 1.6 %copy-done.10 = f32[4096,128]{1,0:T(8,128)S(1)} copy-done((f32[4096,128]{1,0:T(8,128)S(1)}, f32[4096,128]{1,0:T(8,128)}, u32[]{:S(2)}) %copy-start.10) | copy-done | bytes 2097176
  53.5 0.0 copy-start.14
  53.5 0.9 copy-done.14
  54.4 17.1 %shard_map.88 = f32[16,16,128]{2,1,0:T(8,128)} custom-call(s32[1]{0:T(128)} %bitcast.core_ref, bf16[16,64,256]{2,1,0:T(8,128)(2,1)S(1)} %copy-done.3, bf16[16,64,256]{2,1,0:T(8,128)(2,1)S(1)} %copy-done.5, bf16[4096,256]{1,0:T(8,128)(2,1)S(1)} %copy-done.1, f32[4096,128]{1,0:T(8,128)S(1)} %copy-done.10, bf16[16,4096]{1,0:T(8,128)(2,1)S(1)} %copy-done.12, ...), custom_call_target="tpu_custom_call" | custom-call | flops 12884901888 | bytes 8388608 | tf_op jit(solution)/shard_map/pallas_call | solution.py:189
  71.6 0.0 copy-start.8
  71.6 0.0 all-to-all-done.2.mixed_ref
  71.6 6.7 %all-to-all-start.3 = ((f32[16,16,128]{2,1,0:T(8,128)}), f32[16,16,128]{2,1,0:T(8,128)S(1)}, u32[]{:S(2)}, u32[]{:S(2)}) async-start(f32[16,16,128]{2,1,0:T(8,128)} %shard_map.88), calls=%async_computation.3 | async-start | bytes 262144 | tf_op jit(solution)/shard_map/all_to_all | solution.py:257
  78.3 6.7 %all-to-all-done.3.parts_ref = f32[16,16,128]{2,1,0:T(8,128)S(1)} async-done(((f32[16,16,128]{2,1,0:T(8,128)}), f32[16,16,128]{2,1,0:T(8,128)S(1)}, u32[]{:S(2)}, u32[]{:S(2)}) %all-to-all-start.3) | async-done | bytes 131104 | tf_op jit(solution)/shard_map/all_to_all | solution.py:257
  85.0 13.3 %all_to_all.37.parts_ref = f32[16,16,128]{2,1,0:T(8,128)S(1)} all-to-all(f32[16,16,128]{2,1,0:T(8,128)S(1)} %shard_map.91), channel_id=1, replica_groups=mesh['z'=8,'x'=4,'y'=4,'c'=2] {'z','c'}, dimensions={0} | all-to-all | bytes 262144 | tf_op jit(solution)/shard_map/all_to_all | solution.py:257
  98.3 0.2 shard_map.92
  98.5 10.2 %all_to_all.38.parts_ref = f32[16,16,128]{2,1,0:T(8,128)S(1)} all-to-all(f32[16,16,128]{2,1,0:T(8,128)S(1)} %get-tuple-element.19), channel_id=1, replica_groups=mesh['z'=8,'x'=4,'y'=4,'c'=2] {'x','y'}, dimensions={0} | all-to-all | bytes 262144 | tf_op jit(solution)/shard_map/all_to_all | solution.py:257
  108.7 0.7 shard_map.93
  109.4 4.3 %all-to-all-start.6 = ((f32[16,16,128]{2,1,0:T(8,128)}), f32[16,16,128]{2,1,0:T(8,128)S(1)}, u32[]{:S(2)}, u32[]{:S(2)}) async-start(f32[16,16,128]{2,1,0:T(8,128)} %shard_map.93), calls=%async_computation.6 | async-start | bytes 262144 | tf_op jit(solution)/shard_map/all_to_all | solution.py:257
  113.7 0.1 constant_dynamic-slice_fusion
  113.8 0.7 copy.12
  114.5 8.4 %all-to-all-done.6.parts_ref = f32[16,16,128]{2,1,0:T(8,128)S(1)} async-done(((f32[16,16,128]{2,1,0:T(8,128)}), f32[16,16,128]{2,1,0:T(8,128)S(1)}, u32[]{:S(2)}, u32[]{:S(2)}) %all-to-all-start.6) | async-done | bytes 131104 | tf_op jit(solution)/shard_map/all_to_all | solution.py:257
  122.9 0.0 copy-done.8
  122.9 0.7 shard_map.94
  (6 shorter events, 0.1 us)
Async XLA Ops:
  0.6 41.8 %copy-start = (f32[16,8]{0,1:T(8,128)S(1)}, f32[16,8]{0,1:T(8,128)}, u32[]{:S(2)}) copy-start(f32[16,8]{0,1:T(8,128)} %param.9) | copy-start | bytes 1540
  0.6 36.5 %copy-start.1 = (bf16[4096,256]{1,0:T(8,128)(2,1)S(1)}, bf16[4096,256]{1,0:T(8,128)(2,1)}, u32[]{:S(2)}) copy-start(bf16[4096,256]{1,0:T(8,128)(2,1)} %centres_ref.7) | copy-start | bytes 6291460
  0.7 36.5 %copy-start.6 = (f32[16,4096]{1,0:T(8,128)S(1)}, f32[16,4096]{1,0:T(8,128)}, u32[]{:S(2)}) copy-start(f32[16,4096]{1,0:T(8,128)} %weights_ref.1) | copy-start | bytes 786436
  33.9 8.6 %copy-start.2 = (bf16[16,64,256]{2,1,0:T(8,128)(2,1)}, bf16[16,64,256]{2,1,0:T(8,128)(2,1)S(1)}, u32[]{:S(2)}) copy-start(bf16[16,64,256]{2,1,0:T(8,128)(2,1)S(1)} %all_to_all.36.own_ref) | copy-start | bytes 1572868
  33.9 8.6 %collective-permute-start = (bf16[16,64,256]{2,1,0:T(8,128)(2,1)S(1)}, bf16[16,64,256]{2,1,0:T(8,128)(2,1)S(1)}, u32[]{:S(2)}, u32[]{:S(2)}) collective-permute-start(bf16[16,64,256]{2,1,0:T(8,128)(2,1)S(1)} %all_to_all.36.own_ref), channel_id=1, source_target_pairs={{0,1},{1,0},{2,3},{3,2},{4,5},{5,4},{6,7},{7,6},{8,9},{9,8},{10,11... | collective-permute-start | bytes 1572872 | tf_op jit(solution)/shard_map/ppermute | solution.py:290
  37.2 5.4 %copy-start.7 = (f32[64,128]{1,0:T(8,128)S(1)}, f32[64,128]{1,0:T(8,128)}, u32[]{:S(2)}) copy-start(f32[64,128]{1,0:T(8,128)} %vectors_ref.3) | copy-start | bytes 98308
  38.4 1.3 %copy-start.9 = (f32[4096,128]{1,0:T(8,128)}, f32[4096,128]{1,0:T(8,128)S(1)}, u32[]{:S(2)}) copy-start(f32[4096,128]{1,0:T(8,128)S(1)} %get-tuple-element.11.norm_ref) | copy-start | bytes 6291460
  39.8 0.7 copy-start.11
  40.4 0.7 copy-start.13
  42.5 3.7 %copy-start.4 = (bf16[16,64,256]{2,1,0:T(8,128)(2,1)}, bf16[16,64,256]{2,1,0:T(8,128)(2,1)S(1)}, u32[]{:S(2)}) copy-start(bf16[16,64,256]{2,1,0:T(8,128)(2,1)S(1)} %collective-permute-done.other_ref) | copy-start | bytes 1572868
  42.5 7.3 %copy-start.12 = (bf16[16,4096]{1,0:T(8,128)(2,1)S(1)}, bf16[16,4096]{1,0:T(8,128)(2,1)}, u32[]{:S(2)}) copy-start(bf16[16,4096]{1,0:T(8,128)(2,1)} %copy-done.11) | copy-start | bytes 393220
  46.2 25.4 %all-to-all-start.2 = ((f32[16,128,128]{2,1,0:T(8,128)}), f32[16,128,128]{2,1,0:T(8,128)S(1)}, u32[]{:S(2)}, u32[]{:S(2)}) async-start(f32[16,128,128]{2,1,0:T(8,128)} %shard_map.90), calls=%async_computation.2 | async-start | bytes 2097152 | tf_op jit(solution)/shard_map/all_to_all | solution.py:257
  49.9 1.0 copy-start.3
  50.9 1.0 copy-start.5
  51.9 1.6 %copy-start.10 = (f32[4096,128]{1,0:T(8,128)S(1)}, f32[4096,128]{1,0:T(8,128)}, u32[]{:S(2)}) copy-start(f32[4096,128]{1,0:T(8,128)} %copy-done.9) | copy-start | bytes 6291460
  53.5 0.9 copy-start.14
  71.6 51.4 %copy-start.8 = (f32[128]{0:T(128)S(1)}, f32[128]{0:T(128)}, u32[]{:S(2)}) copy-start(f32[128]{0:T(128)} %param.13) | copy-start | bytes 1540
  71.6 13.4 %all-to-all-start.3 = ((f32[16,16,128]{2,1,0:T(8,128)}), f32[16,16,128]{2,1,0:T(8,128)S(1)}, u32[]{:S(2)}, u32[]{:S(2)}) async-start(f32[16,16,128]{2,1,0:T(8,128)} %shard_map.88), calls=%async_computation.3 | async-start | bytes 262144 | tf_op jit(solution)/shard_map/all_to_all | solution.py:257
  109.4 13.5 %all-to-all-start.6 = ((f32[16,16,128]{2,1,0:T(8,128)}), f32[16,16,128]{2,1,0:T(8,128)S(1)}, u32[]{:S(2)}, u32[]{:S(2)}) async-start(f32[16,16,128]{2,1,0:T(8,128)} %shard_map.93), calls=%async_computation.6 | async-start | bytes 262144 | tf_op jit(solution)/shard_map/all_to_all | solution.py:257

commit v4 on v3

--- a/solution.py
+++ b/solution.py
@@ -13,6 +13,7 @@
 PLANE = ("x", "y")
 COLUMN = ("z", "c")
 CHUNK = 256
+PER_STEP = 8
 NT = (((1,), (1,)), ((), ()))
 NN = (((1,), (0,)), ((), ()))
 VMEM_LIMIT = 24 * 1024 * 1024
@@ -145,22 +146,31 @@
 def tile_kernel(
     core_ref, own_ref, other_ref, centres_ref, norm_ref, hi_ref, lo_ref, out_ref,
 ):
-    kernel_values = kernel_of(own_ref, other_ref, range(2))
     both_terms = jnp.concatenate([hi_ref[...], lo_ref[...]], axis=0)
     outputs = hi_ref.shape[0]
-    total = jnp.zeros((2 * outputs, 4 * own_ref.shape[1]), jnp.float32)
-    for base in range(0, centres_ref.shape[0], CHUNK):
-        values = kernel_values(
-            centres_ref[base : base + CHUNK, :], norm_ref[base : base + CHUNK, :]
-        )
-        k_hi = values.astype(jnp.bfloat16)
-        rest = values - k_hi.astype(jnp.float32)
-        terms = both_terms[:, base : base + CHUNK]
-        total = total + mxu(terms, k_hi, NN)
-        total = total + mxu(terms, rest.astype(jnp.bfloat16), NN)
-    predicted = total[:outputs] + total[outputs:]
-    for h in range(2):
-        out_ref[h] = ordered(predicted[:, h * 128 : (h + 1) * 128], core_ref[0])
+
+    def step(start):
+        own_part = own_ref[pl.ds(start, PER_STEP)]
+        other_part = other_ref[pl.ds(start, PER_STEP)]
+        makers = [
+            kernel_of(own_part, other_part, range(h, h + 2)) for h in range(0, PER_STEP, 2)
+        ]
+        for p, kernel_values in enumerate(makers):
+            total = jnp.zeros((2 * outputs, 4 * own_ref.shape[1]), jnp.float32)
+            for base in range(0, centres_ref.shape[0], CHUNK):
+                values = kernel_values(
+                    centres_ref[base : base + CHUNK, :], norm_ref[base : base + CHUNK, :]
+                )
+                k_hi, k_lo = split(values)
+                terms = both_terms[:, base : base + CHUNK]
+                total = total + mxu(terms, k_hi, NN)
+                total = total + mxu(terms, k_lo, NN)
+            predicted = total[:outputs] + total[outputs:]
+            for k in range(2):
+                part = ordered(predicted[:, k * 128 : (k + 1) * 128], core_ref[0])
+                out_ref[start + 2 * p + k] = part
+
+    step(0)
 
 
 def combine_kernel(parts_ref, less_ref, out_ref):
@@ -173,9 +183,11 @@
     out_ref[...] = jnp.broadcast_to(total[None], out_ref.shape)
 
 
-def project_kernel(parts_ref, mixed_ref, residual_ref, out_ref):
+def project_kernel(place_ref, parts_ref, mixed_ref, local_ref, out_ref, turned_ref):
     residual = jnp.sum(parts_ref[...], axis=0)
-    residual_ref[...] = residual
+    own = local_ref.shape[0]
+    turned_ref[...] = residual.T
+    local_ref[...] = turned_ref[pl.ds(pl.multiple_of(place_ref[0] * own, own), own), :]
     projection = dot_f32(residual, jnp.sum(mixed_ref[...], axis=0), NT)
     out_ref[...] = jnp.broadcast_to(projection[None], out_ref.shape)
 
@@ -233,13 +245,13 @@
         in_specs=[vmem] * 2,
         out_specs=(vmem,) * 3,
     )
-    rows_spec = pl.BlockSpec((2, half, depth), lambda i: (i, 0, 0))
+    rows_spec = pl.BlockSpec((PER_STEP, half, depth), lambda i: (i, 0, 0))
     predicted = call(
         tile_kernel, shape((plane, outputs, 128)),
         core, mine, other, centres, norm, w_hi, w_lo,
-        grid=(plane // 2,),
+        grid=(plane // PER_STEP,),
         in_specs=[smem, rows_spec, rows_spec] + [vmem] * 4,
-        out_specs=pl.BlockSpec((2, outputs, 128), lambda i: (i, 0, 0)),
+        out_specs=pl.BlockSpec((PER_STEP, outputs, 128), lambda i: (i, 0, 0)),
         cost_estimate=pl.CostEstimate(
             flops=3 * 2 * count * 2 * plane * half * depth,
             transcendentals=2 * count * 2 * plane * half,
@@ -299,17 +311,19 @@
     summed = exchange(summed, COLUMN)
     residual, projection = call(
         project_kernel,
-        (shape((outputs, 128)), shape((plane, outputs, 128))),
-        summed, mixed,
-    )
-    residual_local = lax.dynamic_slice(residual, (0, place * own), (outputs, own))
+        (shape((own, outputs)), shape((plane, outputs, 128))),
+        place.astype(jnp.int32).reshape(1), summed, mixed,
+        in_specs=[smem, vmem, vmem],
+        out_specs=(vmem, vmem),
+        scratch_shapes=[pltpu.VMEM((128, outputs), jnp.float32)],
+    )
     projection = exchange(projection, PLANE)
     projection = call(spread_kernel, shape((column, outputs, 128)), projection)
     projection = exchange(projection, COLUMN)
     correction = call(
         correct_kernel, shape((outputs, block)), projection, scales[None, :], eigvecs
     )
-    return residual_local, correction
+    return residual.T, correction
 
 
 def solution(mesh):

time: 124 us -> 121 us (0.976)
  blocking collectives: 55 us -> 67.6 us
  waiting for transfers between devices: 15.1 us -> 6.68 us
  starting transfers between devices: 18 us -> 13.6 us
  Pallas kernels: 26.6 us -> 24.2 us
    all_to_all x4 -> x5, blocking collectives: 55 us -> 67.6 us  [exchange(): return lax.all_to_all(x, axes, split_axis=0, concat_axis=0, tiled=True)]
    all_to_all x3 -> x2, waiting for transfers between devices: 15.1 us -> 6.68 us  [exchange(): return lax.all_to_all(x, axes, split_axis=0, concat_axis=0, tiled=True)]
    all_to_all x3 -> x2, starting transfers between devices: 14.7 us -> 10.4 us  [exchange(): return lax.all_to_all(x, axes, split_axis=0, concat_axis=0, tiled=True)]
    pallas_call x9, Pallas kernels: 26.6 us -> 24.2 us  [call(): pl.pallas_call(kernel, out_shape=out, compiler_params=pltpu.CompilerParam...]
    unnamed x31 -> x30, local copies, waits for them, and re-layouts: 7.91 us -> 7.23 us
  transfers between devices with their start and end apart: 4 -> 3, of which waited for: 2 -> 1; matrix products, arithmetic and copies ran while one was open for 1% -> 0% of each run, Pallas kernels for 16% -> 14%
where the time goes in v4:
time: 121 us; the launch traced here: 120 us
  blocking collectives  67.6 us (56%)
  Pallas kernels  24.2 us (20%)
  starting transfers between devices  13.6 us (11%)
  local copies, waits for them, and re-layouts  7.33 us (6%)
  waiting for transfers between devices  6.68 us (6%)
    all_to_all x5, blocking collectives, exchange(): return lax.all_to_all(x, axes, split_axis=0, concat_axis=0, tiled=True)  67.6 us
    pallas_call x9, Pallas kernels, call(): pl.pallas_call(kernel, out_shape=out, compiler_params=pltpu.CompilerParam...  24.2 us
    all_to_all x2, starting transfers between devices, exchange(): return lax.all_to_all(x, axes, split_axis=0, concat_axis=0, tiled=True)  10.4 us
    unnamed x30, local copies, waits for them, and re-layouts  7.23 us
    all_to_all x2, waiting for transfers between devices, exchange(): return lax.all_to_all(x, axes, split_axis=0, concat_axis=0, tiled=True)  6.68 us
    ppermute x1, starting transfers between devices, on_device(): other = lax.ppermute(mine, 'c', [(0, 1), (1, 0)])  3.25 us
  transfers between devices with their start and end apart: 3, of which 1 were waited for; matrix products, arithmetic and copies ran while one was open for 0% of the time, Pallas kernels for 14%

profile of v4, /device:TPU:1, one launch (start us, length us, event | category | flops | bytes accessed | tf_op | source)
XLA Modules:
  0.0 120.3 jit_solution(2179635031288098312)
XLA Ops:
  0.6 0.0 copy-start
  0.6 0.0 copy-start.1
  0.7 0.0 copy-start.6
  0.7 1.7 %shard_map.86 = bf16[8,8,256]{2,1,0:T(8,128)(2,1)S(1)} custom-call(s32[1]{0:T(128)} %bitcast.2.first_ref, s32[8]{0:T(128)} %batch_ref.1, bf16[4096,256]{1,0:T(8,128)(2,1)} %centres_ref.7), custom_call_target="tpu_custom_call" | custom-call | tf_op jit(solution)/shard_map/pallas_call | solution.py:201
  2.4 15.7 %all_to_all.35 = bf16[8,8,256]{2,1,0:T(8,128)(2,1)S(1)} all-to-all(bf16[8,8,256]{2,1,0:T(8,128)(2,1)S(1)} %shard_map.86), channel_id=1, replica_groups=mesh['z'=8,'x'=4,'y'=4,'c'=2] {'z'}, dimensions={0} | all-to-all | bytes 65536 | tf_op jit(solution)/shard_map/all_to_all | solution.py:269
  18.1 15.8 %all_to_all.36.own_ref = bf16[16,64,256]{2,1,0:T(8,128)(2,1)S(1)} all-to-all(bf16[16,64,256]{2,1,0:T(8,128)(2,1)S(1)} %broadcast_in_dim.15), channel_id=1, replica_groups=mesh['z'=8,'x'=4,'y'=4,'c'=2] {'x','y'}, dimensions={0} | all-to-all | bytes 1048576 | tf_op jit(solution)/shard_map/all_to_all | solution.py:269
  33.9 0.0 copy-start.2
  33.9 3.2 %collective-permute-start = (bf16[16,64,256]{2,1,0:T(8,128)(2,1)S(1)}, bf16[16,64,256]{2,1,0:T(8,128)(2,1)S(1)}, u32[]{:S(2)}, u32[]{:S(2)}) collective-permute-start(bf16[16,64,256]{2,1,0:T(8,128)(2,1)S(1)} %all_to_all.36.own_ref), channel_id=1, source_target_pairs={{0,1},{1,0},{2,3},{3,2},{4,5},{5,4},{6,7},{7,6},{8,9},{9,8},{10,11... | collective-permute-start | bytes 1572872 | tf_op jit(solution)/shard_map/ppermute | solution.py:302
  37.1 0.0 copy-done.1
  37.2 0.0 copy-done.6
  37.2 0.0 copy-start.7
  37.2 1.3 %shard_map.87 = (f32[4096,128]{1,0:T(8,128)S(1)}, bf16[16,4096]{1,0:T(8,128)(2,1)S(1)}, bf16[16,4096]{1,0:T(8,128)(2,1)S(1)}) custom-call(bf16[4096,256]{1,0:T(8,128)(2,1)S(1)} %copy-done.1, f32[16,4096]{1,0:T(8,128)S(1)} %copy-done.6), custom_call_target="tpu_custom_call" | custom-call | tf_op jit(solution)/shard_map/pallas_call | solution.py:201
  38.4 0.0 copy-start.9
  38.4 1.3 %copy-done.9 = f32[4096,128]{1,0:T(8,128)} copy-done((f32[4096,128]{1,0:T(8,128)}, f32[4096,128]{1,0:T(8,128)S(1)}, u32[]{:S(2)}) %copy-start.9) | copy-done | bytes 2097176
  39.7 0.0 copy-start.11
  39.7 0.7 copy-done.11
  40.4 0.0 copy-start.13
  40.4 0.7 copy-done.13
  41.0 1.3 %shard_map.89 = (bf16[64,256]{1,0:T(8,128)(2,1)S(1)}, f32[64,128]{1,0:T(8,128)S(1)}) custom-call(s32[1]{0:T(128)} %bitcast.2.first_ref, s32[64]{0:T(128)} %block_ref.1, bf16[4096,256]{1,0:T(8,128)(2,1)S(1)} %copy-done.1), custom_call_target="tpu_custom_call" | custom-call | tf_op jit(solution)/shard_map/pallas_call | solution.py:201
  42.4 0.0 copy-done
  42.4 0.1 copy.10
  42.5 0.0 collective-permute-done.other_ref
  42.5 0.0 copy-start.4
  42.5 0.0 copy-done.2
  42.5 0.0 copy-done.7
  42.5 0.0 copy-start.12
  42.5 3.6 %shard_map.90 = f32[16,128,128]{2,1,0:T(8,128)} custom-call(s32[1]{0:T(128)} %bitcast.1.core_ref, bf16[16,64,256]{2,1,0:T(8,128)(2,1)S(1)} %all_to_all.36.own_ref, bf16[16,64,256]{2,1,0:T(8,128)(2,1)S(1)} %collective-permute-done.other_ref, bf16[64,256]{1,0:T(8,128)(2,1)S(1)} %get-tuple-element.14.points_ref, ...), custom_call_target="tpu_custom_call" | custom-call | tf_op jit(solution)/shard_map/pallas_call | solution.py:201
  46.2 0.0 copy-done.4
  46.2 3.7 %all-to-all-start.2 = ((f32[16,128,128]{2,1,0:T(8,128)}), f32[16,128,128]{2,1,0:T(8,128)S(1)}, u32[]{:S(2)}, u32[]{:S(2)}) async-start(f32[16,128,128]{2,1,0:T(8,128)} %shard_map.90), calls=%async_computation.2 | async-start | bytes 2097152 | tf_op jit(solution)/shard_map/all_to_all | solution.py:269
  49.8 0.0 copy-done.12
  49.8 0.0 copy-start.3
  49.9 1.0 copy-done.3
  50.9 0.0 copy-start.5
  50.9 1.0 copy-done.5
  51.9 0.0 copy-start.10
  51.9 1.6 %copy-done.10 = f32[4096,128]{1,0:T(8,128)S(1)} copy-done((f32[4096,128]{1,0:T(8,128)S(1)}, f32[4096,128]{1,0:T(8,128)}, u32[]{:S(2)}) %copy-start.10) | copy-done | bytes 2097176
  53.5 0.0 copy-start.14
  53.5 0.9 copy-done.14
  54.4 14.8 %shard_map.88 = f32[16,16,128]{2,1,0:T(8,128)} custom-call(s32[1]{0:T(128)} %bitcast.1.core_ref, bf16[16,64,256]{2,1,0:T(8,128)(2,1)S(1)} %copy-done.3, bf16[16,64,256]{2,1,0:T(8,128)(2,1)S(1)} %copy-done.5, bf16[4096,256]{1,0:T(8,128)(2,1)S(1)} %copy-done.1, f32[4096,128]{1,0:T(8,128)S(1)} %copy-done.10, bf16[16,4096]{1,0:T(8,128)(2,1)S(1)} %copy-done.12, ...), custom_call_target="tpu_custom_call" | custom-call | flops 12884901888 | bytes 8388608 | tf_op jit(solution)/shard_map/pallas_call | solution.py:201
  69.2 0.0 copy-start.8
  69.2 0.0 all-to-all-done.2.mixed_ref
  69.2 6.7 %all-to-all-start.3 = ((f32[16,16,128]{2,1,0:T(8,128)}), f32[16,16,128]{2,1,0:T(8,128)S(1)}, u32[]{:S(2)}, u32[]{:S(2)}) async-start(f32[16,16,128]{2,1,0:T(8,128)} %shard_map.88), calls=%async_computation.3 | async-start | bytes 262144 | tf_op jit(solution)/shard_map/all_to_all | solution.py:269
  76.0 6.7 %all-to-all-done.3.parts_ref = f32[16,16,128]{2,1,0:T(8,128)S(1)} async-done(((f32[16,16,128]{2,1,0:T(8,128)}), f32[16,16,128]{2,1,0:T(8,128)S(1)}, u32[]{:S(2)}, u32[]{:S(2)}) %all-to-all-start.3) | async-done | bytes 131104 | tf_op jit(solution)/shard_map/all_to_all | solution.py:269
  82.7 13.3 %all_to_all.37.parts_ref = f32[16,16,128]{2,1,0:T(8,128)S(1)} all-to-all(f32[16,16,128]{2,1,0:T(8,128)S(1)} %shard_map.91), channel_id=1, replica_groups=mesh['z'=8,'x'=4,'y'=4,'c'=2] {'z','c'}, dimensions={0} | all-to-all | bytes 262144 | tf_op jit(solution)/shard_map/all_to_all | solution.py:269
  96.0 0.7 shard_map.92
  96.7 10.2 %all_to_all.38.parts_ref = f32[16,16,128]{2,1,0:T(8,128)S(1)} all-to-all(f32[16,16,128]{2,1,0:T(8,128)S(1)} %get-tuple-element.19), channel_id=1, replica_groups=mesh['z'=8,'x'=4,'y'=4,'c'=2] {'x','y'}, dimensions={0} | all-to-all | bytes 262144 | tf_op jit(solution)/shard_map/all_to_all | solution.py:269
  107.0 12.6 %all_to_all.39.parts_ref = f32[16,16,128]{2,1,0:T(8,128)S(1)} all-to-all(f32[16,16,128]{2,1,0:T(8,128)S(1)} %shard_map.93), channel_id=1, replica_groups=mesh['z'=8,'x'=4,'y'=4,'c'=2] {'z','c'}, dimensions={0} | all-to-all | bytes 262144 | tf_op jit(solution)/shard_map/all_to_all | solution.py:269
  119.6 0.0 copy-done.8
  119.6 0.7 shard_map.94
  (7 shorter events, 0.1 us)
Async XLA Ops:
  0.6 41.8 %copy-start = (f32[16,8]{0,1:T(8,128)S(1)}, f32[16,8]{0,1:T(8,128)}, u32[]{:S(2)}) copy-start(f32[16,8]{0,1:T(8,128)} %param.9) | copy-start | bytes 1540
  0.6 36.5 %copy-start.1 = (bf16[4096,256]{1,0:T(8,128)(2,1)S(1)}, bf16[4096,256]{1,0:T(8,128)(2,1)}, u32[]{:S(2)}) copy-start(bf16[4096,256]{1,0:T(8,128)(2,1)} %centres_ref.7) | copy-start | bytes 6291460
  0.7 36.5 %copy-start.6 = (f32[16,4096]{1,0:T(8,128)S(1)}, f32[16,4096]{1,0:T(8,128)}, u32[]{:S(2)}) copy-start(f32[16,4096]{1,0:T(8,128)} %weights_ref.1) | copy-start | bytes 786436
  33.9 8.6 %copy-start.2 = (bf16[16,64,256]{2,1,0:T(8,128)(2,1)}, bf16[16,64,256]{2,1,0:T(8,128)(2,1)S(1)}, u32[]{:S(2)}) copy-start(bf16[16,64,256]{2,1,0:T(8,128)(2,1)S(1)} %all_to_all.36.own_ref) | copy-start | bytes 1572868
  33.9 8.6 %collective-permute-start = (bf16[16,64,256]{2,1,0:T(8,128)(2,1)S(1)}, bf16[16,64,256]{2,1,0:T(8,128)(2,1)S(1)}, u32[]{:S(2)}, u32[]{:S(2)}) collective-permute-start(bf16[16,64,256]{2,1,0:T(8,128)(2,1)S(1)} %all_to_all.36.own_ref), channel_id=1, source_target_pairs={{0,1},{1,0},{2,3},{3,2},{4,5},{5,4},{6,7},{7,6},{8,9},{9,8},{10,11... | collective-permute-start | bytes 1572872 | tf_op jit(solution)/shard_map/ppermute | solution.py:302
  37.2 5.4 %copy-start.7 = (f32[64,128]{1,0:T(8,128)S(1)}, f32[64,128]{1,0:T(8,128)}, u32[]{:S(2)}) copy-start(f32[64,128]{1,0:T(8,128)} %vectors_ref.3) | copy-start | bytes 98308
  38.4 1.3 %copy-start.9 = (f32[4096,128]{1,0:T(8,128)}, f32[4096,128]{1,0:T(8,128)S(1)}, u32[]{:S(2)}) copy-start(f32[4096,128]{1,0:T(8,128)S(1)} %get-tuple-element.11.norm_ref) | copy-start | bytes 6291460
  39.7 0.7 copy-start.11
  40.4 0.7 copy-start.13
  42.5 3.7 %copy-start.4 = (bf16[16,64,256]{2,1,0:T(8,128)(2,1)}, bf16[16,64,256]{2,1,0:T(8,128)(2,1)S(1)}, u32[]{:S(2)}) copy-start(bf16[16,64,256]{2,1,0:T(8,128)(2,1)S(1)} %collective-permute-done.other_ref) | copy-start | bytes 1572868
  42.5 7.3 %copy-start.12 = (bf16[16,4096]{1,0:T(8,128)(2,1)S(1)}, bf16[16,4096]{1,0:T(8,128)(2,1)}, u32[]{:S(2)}) copy-start(bf16[16,4096]{1,0:T(8,128)(2,1)} %copy-done.11) | copy-start | bytes 393220
  46.2 23.0 %all-to-all-start.2 = ((f32[16,128,128]{2,1,0:T(8,128)}), f32[16,128,128]{2,1,0:T(8,128)S(1)}, u32[]{:S(2)}, u32[]{:S(2)}) async-start(f32[16,128,128]{2,1,0:T(8,128)} %shard_map.90), calls=%async_computation.2 | async-start | bytes 2097152 | tf_op jit(solution)/shard_map/all_to_all | solution.py:269
  49.8 1.0 copy-start.3
  50.9 1.0 copy-start.5
  51.9 1.6 %copy-start.10 = (f32[4096,128]{1,0:T(8,128)S(1)}, f32[4096,128]{1,0:T(8,128)}, u32[]{:S(2)}) copy-start(f32[4096,128]{1,0:T(8,128)} %copy-done.9) | copy-start | bytes 6291460
  53.5 0.9 copy-start.14
  69.2 50.4 %copy-start.8 = (f32[128]{0:T(128)S(1)}, f32[128]{0:T(128)}, u32[]{:S(2)}) copy-start(f32[128]{0:T(128)} %param.13) | copy-start | bytes 1540
  69.2 13.4 %all-to-all-start.3 = ((f32[16,16,128]{2,1,0:T(8,128)}), f32[16,16,128]{2,1,0:T(8,128)S(1)}, u32[]{:S(2)}, u32[]{:S(2)}) async-start(f32[16,16,128]{2,1,0:T(8,128)} %shard_map.88), calls=%async_computation.3 | async-start | bytes 262144 | tf_op jit(solution)/shard_map/all_to_all | solution.py:269

commit v5 on v4

--- a/solution.py
+++ b/solution.py
@@ -210,7 +210,7 @@
     return jax.ShapeDtypeStruct(dims, dtype)
 
 
-def local_part(first, core, centres, mine, other, weights, nystrom_index, eigvecs, move):
+def local_part(first, core, centres, mine, other, weights, nystrom_index, eigvecs, move, less):
     count, depth = centres.shape
     plane, half, _ = mine.shape
     outputs = weights.shape[0]
@@ -227,6 +227,7 @@
         out_specs=(vmem,) * 2,
         scratch_shapes=[pltpu.SMEM((block,), jnp.int32), pltpu.SemaphoreType.DMA(())],
     )
+    points, less = lax.optimization_barrier((points, less))
     mixed = call(
         mixed_kernel, shape((plane, eigen, 128)),
         core, mine, other, points, point_norm, eigvecs,
@@ -258,7 +259,7 @@
             bytes_accessed=8 * count * depth,
         ),
     )
-    return lax.optimization_barrier((predicted, mixed))
+    return (*lax.optimization_barrier((predicted, mixed)), less)
 
 
 def keep(x):
@@ -299,13 +300,14 @@
     )
     rows = exchange(rows, ("z",)).reshape(1, sizes["z"] * own, depth)
     mine = exchange(jnp.broadcast_to(rows, (plane, *rows.shape[1:])), PLANE)
-    other = lax.ppermute(mine, "c", [(0, 1), (1, 0)])
-    predicted, mixed = local_part(
-        first, core, centres, mine, other, weights, nystrom_index, eigvecs,
-        lambda v: exchange(v, PLANE),
-    )
+    mine, targets = lax.optimization_barrier((mine, targets))
     lanes = lax.broadcasted_iota(jnp.int32, (outputs, 128), 1) // own
     less = jnp.where(lanes == place, jnp.tile(targets, (1, 128 // own)), 0.0)
+    other = lax.ppermute(mine, "c", [(0, 1), (1, 0)])
+    predicted, mixed, less = local_part(
+        first, core, centres, mine, other, weights, nystrom_index, eigvecs,
+        lambda v: exchange(v, PLANE), less,
+    )
     gathered = exchange(predicted, PLANE)
     summed = call(combine_kernel, shape((column, outputs, 128)), gathered, less)
     summed = exchange(summed, COLUMN)

time: 121 us -> 118 us (0.975)
  blocking collectives: 67.6 us -> 65.3 us
    all_to_all x5, blocking collectives: 67.6 us -> 65.3 us  [exchange(): return lax.all_to_all(x, axes, split_axis=0, concat_axis=0, tiled=True)]
    all_to_all x2, waiting for transfers between devices: 6.68 us -> 4.62 us  [exchange(): return lax.all_to_all(x, axes, split_axis=0, concat_axis=0, tiled=True)]
    ppermute x1, waiting for transfers between devices: 0.01 us -> 1.45 us  [on_device(): other = lax.ppermute(mine, 'c', [(0, 1), (1, 0)])]
    unnamed x30 -> x26, local copies, waits for them, and re-layouts: 7.23 us -> 6.58 us
  transfers between devices with their start and end apart: 3 -> 3, of which waited for: 1 -> 2; matrix products, arithmetic and copies ran while one was open for 0% -> 0% of each run, Pallas kernels for 14% -> 14%
where the time goes in v5:
time: 118 us; the launch traced here: 117 us
  blocking collectives  65.3 us (55%)
  Pallas kernels  23.6 us (20%)
  starting transfers between devices  13.7 us (12%)
  local copies, waits for them, and re-layouts  7.47 us (6%)
  waiting for transfers between devices  6.08 us (5%)
    all_to_all x5, blocking collectives, exchange(): return lax.all_to_all(x, axes, split_axis=0, concat_axis=0, tiled=True)  65.3 us
    pallas_call x9, Pallas kernels, call(): pl.pallas_call(kernel, out_shape=out, compiler_params=pltpu.CompilerParam...  23.6 us
    all_to_all x2, starting transfers between devices, exchange(): return lax.all_to_all(x, axes, split_axis=0, concat_axis=0, tiled=True)  10.4 us
    unnamed x26, local copies, waits for them, and re-layouts  6.58 us
    all_to_all x2, waiting for transfers between devices, exchange(): return lax.all_to_all(x, axes, split_axis=0, concat_axis=0, tiled=True)  4.62 us
    ppermute x1, starting transfers between devices, on_device(): other = lax.ppermute(mine, 'c', [(0, 1), (1, 0)])  3.25 us
  transfers between devices with their start and end apart: 3, of which 2 were waited for; matrix products, arithmetic and copies ran while one was open for 0% of the time, Pallas kernels for 14%

profile of v5, /device:TPU:1, one launch (start us, length us, event | category | flops | bytes accessed | tf_op | source)
XLA Modules:
  0.0 116.9 jit_solution(2157750701677172315)
XLA Ops:
  0.6 0.0 copy-start
  0.6 0.0 copy-start.1
  0.7 0.0 copy-start.6
  0.7 1.7 %shard_map.86 = bf16[8,8,256]{2,1,0:T(8,128)(2,1)S(1)} custom-call(s32[1]{0:T(128)} %bitcast.2.first_ref, s32[8]{0:T(128)} %batch_ref.1, bf16[4096,256]{1,0:T(8,128)(2,1)} %centres_ref.7), custom_call_target="tpu_custom_call" | custom-call | tf_op jit(solution)/shard_map/pallas_call | solution.py:201
  2.4 15.7 %all_to_all.35 = bf16[8,8,256]{2,1,0:T(8,128)(2,1)S(1)} all-to-all(bf16[8,8,256]{2,1,0:T(8,128)(2,1)S(1)} %shard_map.86), channel_id=1, replica_groups=mesh['z'=8,'x'=4,'y'=4,'c'=2] {'z'}, dimensions={0} | all-to-all | bytes 65536 | tf_op jit(solution)/shard_map/all_to_all | solution.py:270
  18.1 0.8 broadcast_in_dim.15
  18.9 6.8 %all-to-all-start.1 = ((bf16[16,64,256]{2,1,0:T(8,128)(2,1)}), bf16[16,64,256]{2,1,0:T(8,128)(2,1)S(1)}, u32[]{:S(2)}, u32[]{:S(2)}) async-start(bf16[16,64,256]{2,1,0:T(8,128)(2,1)} %broadcast_in_dim.15), calls=%async_computation.1 | async-start | bytes 1048576 | tf_op jit(solution)/shard_map/all_to_all | solution.py:270
  25.7 0.0 copy-done.1
  25.7 0.0 copy-done.6
  25.7 0.0 copy-start.7
  25.7 1.3 %shard_map.87 = (f32[4096,128]{1,0:T(8,128)S(1)}, bf16[16,4096]{1,0:T(8,128)(2,1)S(1)}, bf16[16,4096]{1,0:T(8,128)(2,1)S(1)}) custom-call(bf16[4096,256]{1,0:T(8,128)(2,1)S(1)} %copy-done.1, f32[16,4096]{1,0:T(8,128)S(1)} %copy-done.6), custom_call_target="tpu_custom_call" | custom-call | tf_op jit(solution)/shard_map/pallas_call | solution.py:201
  27.0 0.0 copy-start.9
  27.0 1.3 %copy-done.9 = f32[4096,128]{1,0:T(8,128)} copy-done((f32[4096,128]{1,0:T(8,128)}, f32[4096,128]{1,0:T(8,128)S(1)}, u32[]{:S(2)}) %copy-start.9) | copy-done | bytes 2097176
  28.3 0.0 copy-start.11
  28.3 0.6 copy-done.11
  28.9 1.3 %shard_map.89 = (bf16[64,256]{1,0:T(8,128)(2,1)S(1)}, f32[64,128]{1,0:T(8,128)S(1)}) custom-call(s32[1]{0:T(128)} %bitcast.2.first_ref, s32[64]{0:T(128)} %block_ref.1, bf16[4096,256]{1,0:T(8,128)(2,1)S(1)} %copy-done.1), custom_call_target="tpu_custom_call" | custom-call | tf_op jit(solution)/shard_map/pallas_call | solution.py:201
  30.3 4.6 %all-to-all-done.1.own_ref = bf16[16,64,256]{2,1,0:T(8,128)(2,1)S(1)} async-done(((bf16[16,64,256]{2,1,0:T(8,128)(2,1)}), bf16[16,64,256]{2,1,0:T(8,128)(2,1)S(1)}, u32[]{:S(2)}, u32[]{:S(2)}) %all-to-all-start.1) | async-done | bytes 524320 | tf_op jit(solution)/shard_map/all_to_all | solution.py:270
  34.9 0.0 copy-start.2
  34.9 3.2 %collective-permute-start = (bf16[16,64,256]{2,1,0:T(8,128)(2,1)S(1)}, bf16[16,64,256]{2,1,0:T(8,128)(2,1)S(1)}, u32[]{:S(2)}, u32[]{:S(2)}) collective-permute-start(bf16[16,64,256]{2,1,0:T(8,128)(2,1)S(1)} %all-to-all-done.1.own_ref), channel_id=1, source_target_pairs={{0,1},{1,0},{2,3},{3,2},{4,5},{5,4},{6,7},{7,6},{8,9},{9,8},{10,11... | collective-permute-start | bytes 1572872 | tf_op jit(solution)/shard_map/ppermute | solution.py:306
  38.2 0.0 copy-done
  38.2 0.1 copy.10
  38.2 1.5 %collective-permute-done.other_ref = bf16[16,64,256]{2,1,0:T(8,128)(2,1)S(1)} collective-permute-done((bf16[16,64,256]{2,1,0:T(8,128)(2,1)S(1)}, bf16[16,64,256]{2,1,0:T(8,128)(2,1)S(1)}, u32[]{:S(2)}, u32[]{:S(2)}) %collective-permute-start) | collective-permute-done | bytes 524320 | tf_op jit(solution)/shard_map/ppermute | solution.py:306
  39.7 0.0 copy-start.4
  39.7 0.0 copy-done.7
  39.7 3.6 %shard_map.90 = f32[16,128,128]{2,1,0:T(8,128)} custom-call(s32[1]{0:T(128)} %bitcast.1.core_ref, bf16[16,64,256]{2,1,0:T(8,128)(2,1)S(1)} %all-to-all-done.1.own_ref, bf16[16,64,256]{2,1,0:T(8,128)(2,1)S(1)} %collective-permute-done.other_ref, bf16[64,256]{1,0:T(8,128)(2,1)S(1)} %get-tuple-element.21.points_ref, ...), custom_call_target="tpu_custom_call" | custom-call | tf_op jit(solution)/shard_map/pallas_call | solution.py:201
  43.3 0.0 copy-done.2
  43.3 0.0 copy-done.4
  43.3 3.7 %all-to-all-start.2 = ((f32[16,128,128]{2,1,0:T(8,128)}), f32[16,128,128]{2,1,0:T(8,128)S(1)}, u32[]{:S(2)}, u32[]{:S(2)}) async-start(f32[16,128,128]{2,1,0:T(8,128)} %shard_map.90), calls=%async_computation.2 | async-start | bytes 2097152 | tf_op jit(solution)/shard_map/all_to_all | solution.py:270
  47.0 0.0 copy-start.3
  47.0 1.0 copy-done.3
  48.0 0.0 copy-start.5
  48.0 1.0 copy-done.5
  49.1 0.0 copy-start.10
  49.1 1.6 %copy-done.10 = f32[4096,128]{1,0:T(8,128)S(1)} copy-done((f32[4096,128]{1,0:T(8,128)S(1)}, f32[4096,128]{1,0:T(8,128)}, u32[]{:S(2)}) %copy-start.10) | copy-done | bytes 2097176
  50.7 0.0 copy-start.12
  50.7 0.9 copy-done.12
  51.6 14.2 %shard_map.88 = f32[16,16,128]{2,1,0:T(8,128)S(1)} custom-call(s32[1]{0:T(128)} %bitcast.1.core_ref, bf16[16,64,256]{2,1,0:T(8,128)(2,1)S(1)} %copy-done.3, bf16[16,64,256]{2,1,0:T(8,128)(2,1)S(1)} %copy-done.5, bf16[4096,256]{1,0:T(8,128)(2,1)S(1)} %copy-done.1, f32[4096,128]{1,0:T(8,128)S(1)} %copy-done.10, bf16[16,4096]{1,0:T(8,128)(2,1)S(1)} %get-tuple-element.17.hi_ref, ...), custom_call_target="tpu_custom_call" | custom-call | flops 12884901888 | bytes 8388608 | tf_op jit(solution)/shard_map/pallas_call | solution.py:201
  65.7 0.0 copy-start.8
  65.7 0.0 all-to-all-done.2.mixed_ref
  65.7 13.2 %all_to_all.36.parts_ref = f32[16,16,128]{2,1,0:T(8,128)S(1)} all-to-all(f32[16,16,128]{2,1,0:T(8,128)S(1)} %shard_map.88), channel_id=1, replica_groups=mesh['z'=8,'x'=4,'y'=4,'c'=2] {'x','y'}, dimensions={0} | all-to-all | bytes 262144 | tf_op jit(solution)/shard_map/all_to_all | solution.py:270
  79.0 13.5 %all_to_all.37.parts_ref = f32[16,16,128]{2,1,0:T(8,128)S(1)} all-to-all(f32[16,16,128]{2,1,0:T(8,128)S(1)} %shard_map.91), channel_id=1, replica_groups=mesh['z'=8,'x'=4,'y'=4,'c'=2] {'z','c'}, dimensions={0} | all-to-all | bytes 262144 | tf_op jit(solution)/shard_map/all_to_all | solution.py:270
  92.5 0.7 shard_map.92
  93.3 10.2 %all_to_all.38.parts_ref = f32[16,16,128]{2,1,0:T(8,128)S(1)} all-to-all(f32[16,16,128]{2,1,0:T(8,128)S(1)} %get-tuple-element.27), channel_id=1, replica_groups=mesh['z'=8,'x'=4,'y'=4,'c'=2] {'x','y'}, dimensions={0} | all-to-all | bytes 262144 | tf_op jit(solution)/shard_map/all_to_all | solution.py:270
  103.5 12.6 %all_to_all.39.parts_ref = f32[16,16,128]{2,1,0:T(8,128)S(1)} all-to-all(f32[16,16,128]{2,1,0:T(8,128)S(1)} %shard_map.93), channel_id=1, replica_groups=mesh['z'=8,'x'=4,'y'=4,'c'=2] {'z','c'}, dimensions={0} | all-to-all | bytes 262144 | tf_op jit(solution)/shard_map/all_to_all | solution.py:270
  116.1 0.0 copy-done.8
  116.1 0.7 shard_map.94
  (6 shorter events, 0.1 us)
Async XLA Ops:
  0.6 37.5 %copy-start = (f32[16,8]{0,1:T(8,128)S(1)}, f32[16,8]{0,1:T(8,128)}, u32[]{:S(2)}) copy-start(f32[16,8]{0,1:T(8,128)} %param.9) | copy-start | bytes 1540
  0.6 25.0 %copy-start.1 = (bf16[4096,256]{1,0:T(8,128)(2,1)S(1)}, bf16[4096,256]{1,0:T(8,128)(2,1)}, u32[]{:S(2)}) copy-start(bf16[4096,256]{1,0:T(8,128)(2,1)} %centres_ref.7) | copy-start | bytes 6291460
  0.7 25.0 %copy-start.6 = (f32[16,4096]{1,0:T(8,128)S(1)}, f32[16,4096]{1,0:T(8,128)}, u32[]{:S(2)}) copy-start(f32[16,4096]{1,0:T(8,128)} %weights_ref.1) | copy-start | bytes 786436
  18.9 16.0 %all-to-all-start.1 = ((bf16[16,64,256]{2,1,0:T(8,128)(2,1)}), bf16[16,64,256]{2,1,0:T(8,128)(2,1)S(1)}, u32[]{:S(2)}, u32[]{:S(2)}) async-start(bf16[16,64,256]{2,1,0:T(8,128)(2,1)} %broadcast_in_dim.15), calls=%async_computation.1 | async-start | bytes 1048576 | tf_op jit(solution)/shard_map/all_to_all | solution.py:270
  25.7 14.0 %copy-start.7 = (f32[64,128]{1,0:T(8,128)S(1)}, f32[64,128]{1,0:T(8,128)}, u32[]{:S(2)}) copy-start(f32[64,128]{1,0:T(8,128)} %vectors_ref.3) | copy-start | bytes 98308
  27.0 1.3 %copy-start.9 = (f32[4096,128]{1,0:T(8,128)}, f32[4096,128]{1,0:T(8,128)S(1)}, u32[]{:S(2)}) copy-start(f32[4096,128]{1,0:T(8,128)S(1)} %get-tuple-element.16.norm_ref) | copy-start | bytes 6291460
  28.3 0.6 copy-start.11
  34.9 8.4 %copy-start.2 = (bf16[16,64,256]{2,1,0:T(8,128)(2,1)}, bf16[16,64,256]{2,1,0:T(8,128)(2,1)S(1)}, u32[]{:S(2)}) copy-start(bf16[16,64,256]{2,1,0:T(8,128)(2,1)S(1)} %all-to-all-done.1.own_ref) | copy-start | bytes 1572868
  34.9 4.8 %collective-permute-start = (bf16[16,64,256]{2,1,0:T(8,128)(2,1)S(1)}, bf16[16,64,256]{2,1,0:T(8,128)(2,1)S(1)}, u32[]{:S(2)}, u32[]{:S(2)}) collective-permute-start(bf16[16,64,256]{2,1,0:T(8,128)(2,1)S(1)} %all-to-all-done.1.own_ref), channel_id=1, source_target_pairs={{0,1},{1,0},{2,3},{3,2},{4,5},{5,4},{6,7},{7,6},{8,9},{9,8},{10,11... | collective-permute-start | bytes 1572872 | tf_op jit(solution)/shard_map/ppermute | solution.py:306
  39.7 3.6 %copy-start.4 = (bf16[16,64,256]{2,1,0:T(8,128)(2,1)}, bf16[16,64,256]{2,1,0:T(8,128)(2,1)S(1)}, u32[]{:S(2)}) copy-start(bf16[16,64,256]{2,1,0:T(8,128)(2,1)S(1)} %collective-permute-done.other_ref) | copy-start | bytes 1572868
  43.3 22.4 %all-to-all-start.2 = ((f32[16,128,128]{2,1,0:T(8,128)}), f32[16,128,128]{2,1,0:T(8,128)S(1)}, u32[]{:S(2)}, u32[]{:S(2)}) async-start(f32[16,128,128]{2,1,0:T(8,128)} %shard_map.90), calls=%async_computation.2 | async-start | bytes 2097152 | tf_op jit(solution)/shard_map/all_to_all | solution.py:270
  47.0 1.0 copy-start.3
  48.0 1.0 copy-start.5
  49.1 1.6 %copy-start.10 = (f32[4096,128]{1,0:T(8,128)S(1)}, f32[4096,128]{1,0:T(8,128)}, u32[]{:S(2)}) copy-start(f32[4096,128]{1,0:T(8,128)} %copy-done.9) | copy-start | bytes 6291460
  50.7 0.9 copy-start.12
  65.7 50.4 %copy-start.8 = (f32[128]{0:T(128)S(1)}, f32[128]{0:T(128)}, u32[]{:S(2)}) copy-start(f32[128]{0:T(128)} %param.13) | copy-start | bytes 1540
